TPU v7x, 32 devices: a 4x4x1 block of a 4x4x8 slice. The times are simulated.
32 devices in a mesh: dp: 1 (over z), hp: 4 (over y), sp: 8 (over x, core).
Axes of the slice: x: 4, y: 4, z: 1, core: 2. Of those that a mesh axis runs over, the one named last changes fastest.
The devices are a block of a 4x4x8 slice.
Arguments:
- x_in: bfloat16 [4096, 8192], P(('dp', 'sp', 'hp'))
- w_q: bfloat16 [8192, 8192], P(None, 'hp')
- w_k: bfloat16 [8192, 8192], P(None, 'hp')
- w_v: bfloat16 [8192, 8192], P(None, 'hp')
- w_o: bfloat16 [8192, 8192], P('hp')
Outputs:
- output: bfloat16 [4096, 8192], P(('dp', 'sp', 'hp'))
All inputs are finite; a program needn't handle non-finite values.
Results may differ from a plain program's by a relative error of at most 0.007578.
Values are sent between devices in bfloat16 or wider.
A program may use at most 768 MiB of HBM per device.

v0:
```python
import jax
import jax.numpy as jnp
from jax import lax
from jax.sharding import PartitionSpec as P

HEAD_DIM = 128


def attend_block(q_heads, k_block, v_block, state):
    run_max, run_sum, run_acc = state
    scores = jnp.einsum('qhgd,khd->hgqk', q_heads, k_block, preferred_element_type=jnp.float32) * (HEAD_DIM ** -0.5)
    new_max = jnp.maximum(run_max, jnp.max(scores, axis=-1))
    correction = jnp.exp(run_max - new_max)
    prob_vals = jnp.exp(scores - new_max[..., None])
    new_sum = run_sum * correction + jnp.sum(prob_vals, axis=-1)
    pv_part = jnp.einsum('hgqk,khd->hgqd', prob_vals.astype(jnp.bfloat16), v_block, preferred_element_type=jnp.float32)
    return new_max, new_sum, run_acc * correction[..., None] + pv_part


def solution(mesh):
    seq_ranks = mesh.shape['sp']
    hop_perm = [(source, (source + 1) % seq_ranks) for source in range(seq_ranks)]

    def device_fn(x_loc, w_q, w_k, w_v, w_o):
        x_full = lax.all_gather(x_loc, 'hp', axis=0, tiled=True)
        shard_len = x_full.shape[0]
        head_count = w_q.shape[1] // HEAD_DIM
        kv_count = w_k.shape[1] // HEAD_DIM
        group_size = head_count // kv_count
        q_heads = jnp.dot(x_full, w_q, preferred_element_type=jnp.float32).astype(jnp.bfloat16).reshape(shard_len, kv_count, group_size, HEAD_DIM)
        k_local = jnp.dot(x_full, w_k, preferred_element_type=jnp.float32).astype(jnp.bfloat16).reshape(shard_len, kv_count, HEAD_DIM)
        v_local = jnp.dot(x_full, w_v, preferred_element_type=jnp.float32).astype(jnp.bfloat16).reshape(shard_len, kv_count, HEAD_DIM)
        stat_shape = (kv_count, group_size, shard_len)
        init_state = (jnp.full(stat_shape, -jnp.inf, jnp.float32), jnp.zeros(stat_shape, jnp.float32), jnp.zeros(stat_shape + (HEAD_DIM,), jnp.float32))
        first_state = attend_block(q_heads, k_local, v_local, init_state)

        def hop_step(step_idx, loop_carry):
            k_cur, v_cur, state = loop_carry
            k_cur = lax.ppermute(k_cur, 'sp', hop_perm)
            v_cur = lax.ppermute(v_cur, 'sp', hop_perm)
            return k_cur, v_cur, attend_block(q_heads, k_cur, v_cur, state)

        final_carry = lax.fori_loop(0, seq_ranks - 1, hop_step, (k_local, v_local, first_state))
        run_max, run_sum, run_acc = final_carry[2]
        out_heads = (run_acc / run_sum[..., None]).astype(jnp.bfloat16)
        w_out = w_o.reshape(kv_count, group_size, HEAD_DIM, w_o.shape[1])
        partial_sum = jnp.einsum('hgqd,hgde->qe', out_heads, w_out, preferred_element_type=jnp.float32)
        return lax.psum_scatter(partial_sum, 'hp', scatter_dimension=0, tiled=True).astype(jnp.bfloat16)

    seq_spec = P(('dp', 'sp', 'hp'), None)
    in_specs = (seq_spec, P(None, 'hp'), P(None, 'hp'), P(None, 'hp'), P('hp', None))
    return jax.shard_map(device_fn, mesh=mesh, in_specs=in_specs, out_specs=seq_spec, check_vma=False)
```

profile of v0, /device:TPU:97, one launch (start us, length us, event | category | flops | bytes accessed | tf_op | source)
XLA Modules:
  0.0 819.2 jit_solution(5834316283658543852)
XLA Ops:
  7.4 86.1 %all-gather.2.cloned.1.call-done = bf16[512,8192]{1,0:T(8,128)(2,1)} async-done(((bf16[128,8192]{1,0:T(8,128)(2,1)}), bf16[512,8192]{1,0:T(8,128)(2,1)}) %all-gather.2.cloned.1.call-update) | async-done | bytes 8388624 | tf_op jit(solution)/shard_map/all_gather | solution.py:25
  93.4 25.8 %convolution_convert_fusion = bf16[512,2048]{1,0:T(8,128)(2,1)S(1)} fusion(bf16[512,8192]{1,0:T(8,128)(2,1)} %all-gather.2.cloned.1.call-done, bf16[8192,2048]{1,0:T(8,128)(2,1)} %param.8), kind=kOutput, calls=%fused_computation.29 | convolution fusion | flops 17180917760 | bytes 44040192 | tf_op jit(solution)/shard_map/dot_general | solution.py:30
  119.3 22.1 %fusion.28 = bf16[64,16,8,128]{3,2,1,0:T(8,128)(2,1)S(1)} fusion(bf16[512,8192]{1,0:T(8,128)(2,1)S(1)} %copy-done.7, bf16[8192,2048]{1,0:T(8,128)(2,1)} %param.9), kind=kOutput, calls=%fused_computation.38 | convolution fusion | flops 17180917760 | bytes 44040192 | tf_op jit(solution)/shard_map/dot_general | solution.py:31
  148.8 8.7 %fusion.16 = f32[16,512]{1,0:T(8,128)S(1)} fusion(f32[16,512,512]{2,1,0:T(8,128)} %get-tuple-element.71, f32[16,512]{1,0:T(8,128)S(1)} %get-tuple-element.70), kind=kLoop, calls=%fused_computation.21 | loop fusion | flops 12574720 | bytes 16842752 | tf_op jit(solution)/shard_map/reduce_sum | solution.py:15
  157.5 24.1 %fusion.29 = bf16[64,16,8,128]{3,2,1,0:T(8,128)(2,1)S(1)} fusion(bf16[512,8192]{1,0:T(8,128)(2,1)} %all-gather.2.cloned.1.call-done, bf16[8192,2048]{1,0:T(8,128)(2,1)} %param.10), kind=kOutput, calls=%fused_computation.39 | convolution fusion | flops 17180917760 | bytes 44040192 | tf_op jit(solution)/shard_map/dot_general | solution.py:32
  196.2 434.0 %while.18 = (s32[]{:T(128)}, bf16[512,16,128]{2,0,1:T(8,128)(2,1)}, bf16[512,16,128]{2,0,1:T(8,128)(2,1)}, f32[16,1,512]{2,0,1:T(8,128)S(1)}, f32[16,1,512]{2,0,...) while((s32[]{:T(128)}, bf16[512,16,128]{2,0,1:T(8,128)(2,1)}, ...), condition=%wide.region_5.0_spmd, body=%wide.region_2.0_spmd.sunk | while | flops 2183159808 | bytes 124256480 | solution.py:43
  198.2 22.9 %collective-permute-done = bf16[512,16,128]{2,0,1:T(8,128)(2,1)S(1)} collective-permute-done((bf16[512,16,128]{2,0,1:T(8,128)(2,1)}, bf16[512,16,128]{2,0,1:T(8,128)(2,1)S(1)}, u32[]{:S(2)}, u32[]{:S(2)}) %collective-permute-start) | collective-permute-done | bytes 2097184 | tf_op jit(solution)/shard_map/while/body/eval_jaxpr/ppermute | solution.py:39
  221.2 9.7 %bitcast_reduce_fusion.3 = (f32[16,512]{1,0:T(8,128)S(1)}, f32[16,512,512]{2,1,0:T(8,128)}) fusion(bf16[512,16,128]{2,0,1:T(8,128)(2,1)S(1)} %collective-permute-done, bf16[512,16,1,128]{3,0,1,2:T(8,128)(2,1)} %get-tuple-element.147), kind=kOutput, calls=%fused_computation.1.clone.1 | convolution fusion | flops 1082122240 | bytes 21004288 | tf_op jit(solution)/shard_map/while/body/eval_jaxpr/qhgd,khd->hgqk/dot_general | solution.py:11
  230.9 8.6 %fusion.50 = f32[16,512]{1,0:T(8,128)S(1)} fusion(f32[16,512,512]{2,1,0:T(8,128)} %get-tuple-element.123, f32[16,512]{1,0:T(8,128)S(1)} %bitcast.128), kind=kLoop, calls=%fused_computation.4.clone.1 | loop fusion | flops 12574720 | bytes 16842752 | tf_op jit(solution)/shard_map/while/body/eval_jaxpr/reduce_sum | solution.py:15
  246.8 9.0 %bitcast_add_fusion.6 = f32[16,1,512,128]{3,2,0,1:T(8,128)S(1)} fusion(f32[16,1,512,128]{3,2,0,1:T(8,128)S(1)} %copy-done, bf16[512,16,128]{2,0,1:T(8,128)(2,1)} %collective-permute-done.1, f32[16,512,512]{2,1,0:T(8,128)} %get-tuple-element.123, f32[16,512]{1,0:T(8,128)S(1)} %bitcast.129, f32[16,512]{1,0:T(8,128)S(1)} %get-tuple-element.124), kind=kOutput, calls=%fused_computation.9.clone.1 | convolution fusion | flops 1088421888 | bytes 27328512 | tf_op jit(solution)/shard_map/while/body/eval_jaxpr/hgqk,khd->hgqd/dot_general | solution.py:16
  260.3 22.9 %collective-permute-done = bf16[512,16,128]{2,0,1:T(8,128)(2,1)S(1)} collective-permute-done((bf16[512,16,128]{2,0,1:T(8,128)(2,1)}, bf16[512,16,128]{2,0,1:T(8,128)(2,1)S(1)}, u32[]{:S(2)}, u32[]{:S(2)}) %collective-permute-start) | collective-permute-done | bytes 2097184 | tf_op jit(solution)/shard_map/while/body/eval_jaxpr/ppermute | solution.py:39
  283.2 9.7 %bitcast_reduce_fusion.3 = (f32[16,512]{1,0:T(8,128)S(1)}, f32[16,512,512]{2,1,0:T(8,128)}) fusion(bf16[512,16,128]{2,0,1:T(8,128)(2,1)S(1)} %collective-permute-done, bf16[512,16,1,128]{3,0,1,2:T(8,128)(2,1)} %get-tuple-element.147), kind=kOutput, calls=%fused_computation.1.clone.1 | convolution fusion | flops 1082122240 | bytes 21004288 | tf_op jit(solution)/shard_map/while/body/eval_jaxpr/qhgd,khd->hgqk/dot_general | solution.py:11
  292.9 8.6 %fusion.50 = f32[16,512]{1,0:T(8,128)S(1)} fusion(f32[16,512,512]{2,1,0:T(8,128)} %get-tuple-element.123, f32[16,512]{1,0:T(8,128)S(1)} %bitcast.128), kind=kLoop, calls=%fused_computation.4.clone.1 | loop fusion | flops 12574720 | bytes 16842752 | tf_op jit(solution)/shard_map/while/body/eval_jaxpr/reduce_sum | solution.py:15
  308.8 9.0 %bitcast_add_fusion.6 = f32[16,1,512,128]{3,2,0,1:T(8,128)S(1)} fusion(f32[16,1,512,128]{3,2,0,1:T(8,128)S(1)} %copy-done, bf16[512,16,128]{2,0,1:T(8,128)(2,1)} %collective-permute-done.1, f32[16,512,512]{2,1,0:T(8,128)} %get-tuple-element.123, f32[16,512]{1,0:T(8,128)S(1)} %bitcast.129, f32[16,512]{1,0:T(8,128)S(1)} %get-tuple-element.124), kind=kOutput, calls=%fused_computation.9.clone.1 | convolution fusion | flops 1088421888 | bytes 27328512 | tf_op jit(solution)/shard_map/while/body/eval_jaxpr/hgqk,khd->hgqd/dot_general | solution.py:16
  322.4 22.9 %collective-permute-done = bf16[512,16,128]{2,0,1:T(8,128)(2,1)S(1)} collective-permute-done((bf16[512,16,128]{2,0,1:T(8,128)(2,1)}, bf16[512,16,128]{2,0,1:T(8,128)(2,1)S(1)}, u32[]{:S(2)}, u32[]{:S(2)}) %collective-permute-start) | collective-permute-done | bytes 2097184 | tf_op jit(solution)/shard_map/while/body/eval_jaxpr/ppermute | solution.py:39
  345.3 9.7 %bitcast_reduce_fusion.3 = (f32[16,512]{1,0:T(8,128)S(1)}, f32[16,512,512]{2,1,0:T(8,128)}) fusion(bf16[512,16,128]{2,0,1:T(8,128)(2,1)S(1)} %collective-permute-done, bf16[512,16,1,128]{3,0,1,2:T(8,128)(2,1)} %get-tuple-element.147), kind=kOutput, calls=%fused_computation.1.clone.1 | convolution fusion | flops 1082122240 | bytes 21004288 | tf_op jit(solution)/shard_map/while/body/eval_jaxpr/qhgd,khd->hgqk/dot_general | solution.py:11
  355.0 8.6 %fusion.50 = f32[16,512]{1,0:T(8,128)S(1)} fusion(f32[16,512,512]{2,1,0:T(8,128)} %get-tuple-element.123, f32[16,512]{1,0:T(8,128)S(1)} %bitcast.128), kind=kLoop, calls=%fused_computation.4.clone.1 | loop fusion | flops 12574720 | bytes 16842752 | tf_op jit(solution)/shard_map/while/body/eval_jaxpr/reduce_sum | solution.py:15
  370.9 9.0 %bitcast_add_fusion.6 = f32[16,1,512,128]{3,2,0,1:T(8,128)S(1)} fusion(f32[16,1,512,128]{3,2,0,1:T(8,128)S(1)} %copy-done, bf16[512,16,128]{2,0,1:T(8,128)(2,1)} %collective-permute-done.1, f32[16,512,512]{2,1,0:T(8,128)} %get-tuple-element.123, f32[16,512]{1,0:T(8,128)S(1)} %bitcast.129, f32[16,512]{1,0:T(8,128)S(1)} %get-tuple-element.124), kind=kOutput, calls=%fused_computation.9.clone.1 | convolution fusion | flops 1088421888 | bytes 27328512 | tf_op jit(solution)/shard_map/while/body/eval_jaxpr/hgqk,khd->hgqd/dot_general | solution.py:16
  384.4 22.9 %collective-permute-done = bf16[512,16,128]{2,0,1:T(8,128)(2,1)S(1)} collective-permute-done((bf16[512,16,128]{2,0,1:T(8,128)(2,1)}, bf16[512,16,128]{2,0,1:T(8,128)(2,1)S(1)}, u32[]{:S(2)}, u32[]{:S(2)}) %collective-permute-start) | collective-permute-done | bytes 2097184 | tf_op jit(solution)/shard_map/while/body/eval_jaxpr/ppermute | solution.py:39
  407.4 9.7 %bitcast_reduce_fusion.3 = (f32[16,512]{1,0:T(8,128)S(1)}, f32[16,512,512]{2,1,0:T(8,128)}) fusion(bf16[512,16,128]{2,0,1:T(8,128)(2,1)S(1)} %collective-permute-done, bf16[512,16,1,128]{3,0,1,2:T(8,128)(2,1)} %get-tuple-element.147), kind=kOutput, calls=%fused_computation.1.clone.1 | convolution fusion | flops 1082122240 | bytes 21004288 | tf_op jit(solution)/shard_map/while/body/eval_jaxpr/qhgd,khd->hgqk/dot_general | solution.py:11
  433.0 9.0 %bitcast_add_fusion.6 = f32[16,1,512,128]{3,2,0,1:T(8,128)S(1)} fusion(f32[16,1,512,128]{3,2,0,1:T(8,128)S(1)} %copy-done, bf16[512,16,128]{2,0,1:T(8,128)(2,1)} %collective-permute-done.1, f32[16,512,512]{2,1,0:T(8,128)} %get-tuple-element.123, f32[16,512]{1,0:T(8,128)S(1)} %bitcast.129, f32[16,512]{1,0:T(8,128)S(1)} %get-tuple-element.124), kind=kOutput, calls=%fused_computation.9.clone.1 | convolution fusion | flops 1088421888 | bytes 27328512 | tf_op jit(solution)/shard_map/while/body/eval_jaxpr/hgqk,khd->hgqd/dot_general | solution.py:16
  446.5 22.9 %collective-permute-done = bf16[512,16,128]{2,0,1:T(8,128)(2,1)S(1)} collective-permute-done((bf16[512,16,128]{2,0,1:T(8,128)(2,1)}, bf16[512,16,128]{2,0,1:T(8,128)(2,1)S(1)}, u32[]{:S(2)}, u32[]{:S(2)}) %collective-permute-start) | collective-permute-done | bytes 2097184 | tf_op jit(solution)/shard_map/while/body/eval_jaxpr/ppermute | solution.py:39
  469.4 9.7 %bitcast_reduce_fusion.3 = (f32[16,512]{1,0:T(8,128)S(1)}, f32[16,512,512]{2,1,0:T(8,128)}) fusion(bf16[512,16,128]{2,0,1:T(8,128)(2,1)S(1)} %collective-permute-done, bf16[512,16,1,128]{3,0,1,2:T(8,128)(2,1)} %get-tuple-element.147), kind=kOutput, calls=%fused_computation.1.clone.1 | convolution fusion | flops 1082122240 | bytes 21004288 | tf_op jit(solution)/shard_map/while/body/eval_jaxpr/qhgd,khd->hgqk/dot_general | solution.py:11
  495.1 9.0 %bitcast_add_fusion.6 = f32[16,1,512,128]{3,2,0,1:T(8,128)S(1)} fusion(f32[16,1,512,128]{3,2,0,1:T(8,128)S(1)} %copy-done, bf16[512,16,128]{2,0,1:T(8,128)(2,1)} %collective-permute-done.1, f32[16,512,512]{2,1,0:T(8,128)} %get-tuple-element.123, f32[16,512]{1,0:T(8,128)S(1)} %bitcast.129, f32[16,512]{1,0:T(8,128)S(1)} %get-tuple-element.124), kind=kOutput, calls=%fused_computation.9.clone.1 | convolution fusion | flops 1088421888 | bytes 27328512 | tf_op jit(solution)/shard_map/while/body/eval_jaxpr/hgqk,khd->hgqd/dot_general | solution.py:16
  508.6 22.9 %collective-permute-done = bf16[512,16,128]{2,0,1:T(8,128)(2,1)S(1)} collective-permute-done((bf16[512,16,128]{2,0,1:T(8,128)(2,1)}, bf16[512,16,128]{2,0,1:T(8,128)(2,1)S(1)}, u32[]{:S(2)}, u32[]{:S(2)}) %collective-permute-start) | collective-permute-done | bytes 2097184 | tf_op jit(solution)/shard_map/while/body/eval_jaxpr/ppermute | solution.py:39
  531.5 9.7 %bitcast_reduce_fusion.3 = (f32[16,512]{1,0:T(8,128)S(1)}, f32[16,512,512]{2,1,0:T(8,128)}) fusion(bf16[512,16,128]{2,0,1:T(8,128)(2,1)S(1)} %collective-permute-done, bf16[512,16,1,128]{3,0,1,2:T(8,128)(2,1)} %get-tuple-element.147), kind=kOutput, calls=%fused_computation.1.clone.1 | convolution fusion | flops 1082122240 | bytes 21004288 | tf_op jit(solution)/shard_map/while/body/eval_jaxpr/qhgd,khd->hgqk/dot_general | solution.py:11
  557.1 9.0 %bitcast_add_fusion.6 = f32[16,1,512,128]{3,2,0,1:T(8,128)S(1)} fusion(f32[16,1,512,128]{3,2,0,1:T(8,128)S(1)} %copy-done, bf16[512,16,128]{2,0,1:T(8,128)(2,1)} %collective-permute-done.1, f32[16,512,512]{2,1,0:T(8,128)} %get-tuple-element.123, f32[16,512]{1,0:T(8,128)S(1)} %bitcast.129, f32[16,512]{1,0:T(8,128)S(1)} %get-tuple-element.124), kind=kOutput, calls=%fused_computation.9.clone.1 | convolution fusion | flops 1088421888 | bytes 27328512 | tf_op jit(solution)/shard_map/while/body/eval_jaxpr/hgqk,khd->hgqd/dot_general | solution.py:16
  570.6 22.9 %collective-permute-done = bf16[512,16,128]{2,0,1:T(8,128)(2,1)S(1)} collective-permute-done((bf16[512,16,128]{2,0,1:T(8,128)(2,1)}, bf16[512,16,128]{2,0,1:T(8,128)(2,1)S(1)}, u32[]{:S(2)}, u32[]{:S(2)}) %collective-permute-start) | collective-permute-done | bytes 2097184 | tf_op jit(solution)/shard_map/while/body/eval_jaxpr/ppermute | solution.py:39
  593.6 9.7 %bitcast_reduce_fusion.3 = (f32[16,512]{1,0:T(8,128)S(1)}, f32[16,512,512]{2,1,0:T(8,128)}) fusion(bf16[512,16,128]{2,0,1:T(8,128)(2,1)S(1)} %collective-permute-done, bf16[512,16,1,128]{3,0,1,2:T(8,128)(2,1)} %get-tuple-element.147), kind=kOutput, calls=%fused_computation.1.clone.1 | convolution fusion | flops 1082122240 | bytes 21004288 | tf_op jit(solution)/shard_map/while/body/eval_jaxpr/qhgd,khd->hgqk/dot_general | solution.py:11
  619.2 9.0 %bitcast_add_fusion.6 = f32[16,1,512,128]{3,2,0,1:T(8,128)S(1)} fusion(f32[16,1,512,128]{3,2,0,1:T(8,128)S(1)} %copy-done, bf16[512,16,128]{2,0,1:T(8,128)(2,1)} %collective-permute-done.1, f32[16,512,512]{2,1,0:T(8,128)} %get-tuple-element.123, f32[16,512]{1,0:T(8,128)S(1)} %bitcast.129, f32[16,512]{1,0:T(8,128)S(1)} %get-tuple-element.124), kind=kOutput, calls=%fused_computation.9.clone.1 | convolution fusion | flops 1088421888 | bytes 27328512 | tf_op jit(solution)/shard_map/while/body/eval_jaxpr/hgqk,khd->hgqd/dot_general | solution.py:16
  630.2 25.3 %convolution_bitcast_fusion = f32[512,8192]{1,0:T(8,128)} fusion(bf16[16,128,8192]{2,1,0:T(8,128)(2,1)} %bitcast.134, f32[16,1,512,128]{3,2,0,1:T(8,128)} %get-tuple-element.43, f32[16,512]{1,0:T(8,128)S(1)} %bitcast.133), kind=kOutput, calls=%fused_computation.22 | convolution fusion | flops 17181966336 | bytes 54558720 | tf_op jit(solution)/shard_map/hgqd,hgde->qe/dot_general | solution.py:47
  655.5 153.0 %reduce-scatter.2.cloned.1.call-done = f32[128,8192]{1,0:T(8,128)} async-done(((f32[512,8192]{1,0:T(8,128)}), f32[128,8192]{1,0:T(8,128)}) %reduce-scatter.2.cloned.1.call-update) | async-done | bytes 4194320 | tf_op jit(solution)/shard_map/reduce_scatter | solution.py:48
  (121 shorter events, 142.8 us)
Async XLA Ops:
  6.5 86.9 %all-gather.2.cloned.1.call-start = ((), (), s32[]{:S(2)}) async-start(), calls=%async_computation.1 | async-start | bytes 10485760 | tf_op jit(solution)/shard_map/all_gather | solution.py:25
  7.3 801.2 %reduce-scatter.2.cloned.1.call-start = ((), (), s32[]{:S(2)}) async-start(), calls=%async_computation.2 | async-start | bytes 20971520 | tf_op jit(solution)/shard_map/reduce_scatter | solution.py:48
  93.4 25.8 %copy-start.7 = (bf16[512,8192]{1,0:T(8,128)(2,1)S(1)}, bf16[512,8192]{1,0:T(8,128)(2,1)}, u32[]{:S(2)}) copy-start(bf16[512,8192]{1,0:T(8,128)(2,1)} %all-gather.2.cloned.1.call-done) | copy-start | bytes 25165828
  119.3 22.2 %copy-start.2 = (bf16[512,2048]{1,0:T(8,128)(2,1)}, bf16[512,2048]{1,0:T(8,128)(2,1)S(1)}, u32[]{:S(2)}) copy-start(bf16[512,2048]{1,0:T(8,128)(2,1)S(1)} %convolution_convert_fusion) | copy-start | bytes 6291460
  141.5 7.3 copy-start.4
  148.8 37.4 %slice-start = ((s8[16777216]{0:T(1024)(128)(4,1)}), s8[4194304]{0:T(1024)(128)(4,1)S(1)}, s32[]{:S(2)}) async-start(s8[16777216]{0:T(1024)(128)(4,1)} %bitcast.126), calls=%async_computation.3 | async-start | bytes 8388608
  157.5 25.5 %copy-start.5 = (bf16[64,16,8,128]{3,2,1,0:T(8,128)(2,1)S(1)}, bf16[64,16,8,128]{3,2,1,0:T(8,128)(2,1)}, u32[]{:S(2)}) copy-start(bf16[64,16,8,128]{3,2,1,0:T(8,128)(2,1)} %copy-done.4) | copy-start | bytes 6291460
  157.5 28.6 %slice-start.1 = ((s8[16777216]{0:T(1024)(128)(4,1)}), s8[4194304]{0:T(1024)(128)(4,1)S(1)}, s32[]{:S(2)}) async-start(s8[16777216]{0:T(1024)(128)(4,1)} %bitcast.126), calls=%async_computation.4 | async-start | bytes 8388608
  157.5 28.6 %slice-start.2 = ((s8[16777216]{0:T(1024)(128)(4,1)}), s8[4194304]{0:T(1024)(128)(4,1)S(1)}, s32[]{:S(2)}) async-start(s8[16777216]{0:T(1024)(128)(4,1)} %bitcast.126), calls=%async_computation.5 | async-start | bytes 8388608
  157.5 28.6 %slice-start.3 = ((s8[16777216]{0:T(1024)(128)(4,1)}), s8[4194304]{0:T(1024)(128)(4,1)S(1)}, s32[]{:S(2)}) async-start(s8[16777216]{0:T(1024)(128)(4,1)} %bitcast.126), calls=%async_computation.6 | async-start | bytes 8388608
  186.2 7.5 copy-start.3
  196.2 25.0 %collective-permute-start = (bf16[512,16,128]{2,0,1:T(8,128)(2,1)}, bf16[512,16,128]{2,0,1:T(8,128)(2,1)S(1)}, u32[]{:S(2)}, u32[]{:S(2)}) collective-permute-start(bf16[512,16,128]{2,0,1:T(8,128)(2,1)} %get-tuple-element.134), channel_id=1, source_target_pairs={{0,1},{1,2},{2,3},{3,4},{4,5},{5,6},{6,7},{7,0},{8,9},{9,10},{10,1... | collective-permute-start | bytes 6291464 | tf_op jit(solution)/shard_map/while/body/eval_jaxpr/ppermute | solution.py:39
  198.2 45.4 %collective-permute-start.1 = (bf16[512,16,128]{2,0,1:T(8,128)(2,1)}, bf16[512,16,128]{2,0,1:T(8,128)(2,1)}, u32[]{:S(2)}, u32[]{:S(2)}) collective-permute-start(bf16[512,16,128]{2,0,1:T(8,128)(2,1)} %get-tuple-element.135), channel_id=1, source_target_pairs={{0,1},{1,2},{2,3},{3,4},{4,5},{5,6},{6,7},{7,0},{8,9},{9,10},{10,1... | collective-permute-start | bytes 6291464 | tf_op jit(solution)/shard_map/while/body/eval_jaxpr/ppermute | solution.py:40
  239.4 7.3 copy-start
  257.8 25.5 %collective-permute-start = (bf16[512,16,128]{2,0,1:T(8,128)(2,1)}, bf16[512,16,128]{2,0,1:T(8,128)(2,1)S(1)}, u32[]{:S(2)}, u32[]{:S(2)}) collective-permute-start(bf16[512,16,128]{2,0,1:T(8,128)(2,1)} %get-tuple-element.134), channel_id=1, source_target_pairs={{0,1},{1,2},{2,3},{3,4},{4,5},{5,6},{6,7},{7,0},{8,9},{9,10},{10,1... | collective-permute-start | bytes 6291464 | tf_op jit(solution)/shard_map/while/body/eval_jaxpr/ppermute | solution.py:39
  260.3 45.4 %collective-permute-start.1 = (bf16[512,16,128]{2,0,1:T(8,128)(2,1)}, bf16[512,16,128]{2,0,1:T(8,128)(2,1)}, u32[]{:S(2)}, u32[]{:S(2)}) collective-permute-start(bf16[512,16,128]{2,0,1:T(8,128)(2,1)} %get-tuple-element.135), channel_id=1, source_target_pairs={{0,1},{1,2},{2,3},{3,4},{4,5},{5,6},{6,7},{7,0},{8,9},{9,10},{10,1... | collective-permute-start | bytes 6291464 | tf_op jit(solution)/shard_map/while/body/eval_jaxpr/ppermute | solution.py:40
  301.5 7.3 copy-start
  319.8 25.5 %collective-permute-start = (bf16[512,16,128]{2,0,1:T(8,128)(2,1)}, bf16[512,16,128]{2,0,1:T(8,128)(2,1)S(1)}, u32[]{:S(2)}, u32[]{:S(2)}) collective-permute-start(bf16[512,16,128]{2,0,1:T(8,128)(2,1)} %get-tuple-element.134), channel_id=1, source_target_pairs={{0,1},{1,2},{2,3},{3,4},{4,5},{5,6},{6,7},{7,0},{8,9},{9,10},{10,1... | collective-permute-start | bytes 6291464 | tf_op jit(solution)/shard_map/while/body/eval_jaxpr/ppermute | solution.py:39
  322.3 45.4 %collective-permute-start.1 = (bf16[512,16,128]{2,0,1:T(8,128)(2,1)}, bf16[512,16,128]{2,0,1:T(8,128)(2,1)}, u32[]{:S(2)}, u32[]{:S(2)}) collective-permute-start(bf16[512,16,128]{2,0,1:T(8,128)(2,1)} %get-tuple-element.135), channel_id=1, source_target_pairs={{0,1},{1,2},{2,3},{3,4},{4,5},{5,6},{6,7},{7,0},{8,9},{9,10},{10,1... | collective-permute-start | bytes 6291464 | tf_op jit(solution)/shard_map/while/body/eval_jaxpr/ppermute | solution.py:40
  363.6 7.3 copy-start
  381.9 25.5 %collective-permute-start = (bf16[512,16,128]{2,0,1:T(8,128)(2,1)}, bf16[512,16,128]{2,0,1:T(8,128)(2,1)S(1)}, u32[]{:S(2)}, u32[]{:S(2)}) collective-permute-start(bf16[512,16,128]{2,0,1:T(8,128)(2,1)} %get-tuple-element.134), channel_id=1, source_target_pairs={{0,1},{1,2},{2,3},{3,4},{4,5},{5,6},{6,7},{7,0},{8,9},{9,10},{10,1... | collective-permute-start | bytes 6291464 | tf_op jit(solution)/shard_map/while/body/eval_jaxpr/ppermute | solution.py:39
  384.4 45.4 %collective-permute-start.1 = (bf16[512,16,128]{2,0,1:T(8,128)(2,1)}, bf16[512,16,128]{2,0,1:T(8,128)(2,1)}, u32[]{:S(2)}, u32[]{:S(2)}) collective-permute-start(bf16[512,16,128]{2,0,1:T(8,128)(2,1)} %get-tuple-element.135), channel_id=1, source_target_pairs={{0,1},{1,2},{2,3},{3,4},{4,5},{5,6},{6,7},{7,0},{8,9},{9,10},{10,1... | collective-permute-start | bytes 6291464 | tf_op jit(solution)/shard_map/while/body/eval_jaxpr/ppermute | solution.py:40
  425.7 7.3 copy-start
  444.0 25.5 %collective-permute-start = (bf16[512,16,128]{2,0,1:T(8,128)(2,1)}, bf16[512,16,128]{2,0,1:T(8,128)(2,1)S(1)}, u32[]{:S(2)}, u32[]{:S(2)}) collective-permute-start(bf16[512,16,128]{2,0,1:T(8,128)(2,1)} %get-tuple-element.134), channel_id=1, source_target_pairs={{0,1},{1,2},{2,3},{3,4},{4,5},{5,6},{6,7},{7,0},{8,9},{9,10},{10,1... | collective-permute-start | bytes 6291464 | tf_op jit(solution)/shard_map/while/body/eval_jaxpr/ppermute | solution.py:39
  446.5 45.4 %collective-permute-start.1 = (bf16[512,16,128]{2,0,1:T(8,128)(2,1)}, bf16[512,16,128]{2,0,1:T(8,128)(2,1)}, u32[]{:S(2)}, u32[]{:S(2)}) collective-permute-start(bf16[512,16,128]{2,0,1:T(8,128)(2,1)} %get-tuple-element.135), channel_id=1, source_target_pairs={{0,1},{1,2},{2,3},{3,4},{4,5},{5,6},{6,7},{7,0},{8,9},{9,10},{10,1... | collective-permute-start | bytes 6291464 | tf_op jit(solution)/shard_map/while/body/eval_jaxpr/ppermute | solution.py:40
  487.7 7.3 copy-start
  506.1 25.5 %collective-permute-start = (bf16[512,16,128]{2,0,1:T(8,128)(2,1)}, bf16[512,16,128]{2,0,1:T(8,128)(2,1)S(1)}, u32[]{:S(2)}, u32[]{:S(2)}) collective-permute-start(bf16[512,16,128]{2,0,1:T(8,128)(2,1)} %get-tuple-element.134), channel_id=1, source_target_pairs={{0,1},{1,2},{2,3},{3,4},{4,5},{5,6},{6,7},{7,0},{8,9},{9,10},{10,1... | collective-permute-start | bytes 6291464 | tf_op jit(solution)/shard_map/while/body/eval_jaxpr/ppermute | solution.py:39
  508.6 45.4 %collective-permute-start.1 = (bf16[512,16,128]{2,0,1:T(8,128)(2,1)}, bf16[512,16,128]{2,0,1:T(8,128)(2,1)}, u32[]{:S(2)}, u32[]{:S(2)}) collective-permute-start(bf16[512,16,128]{2,0,1:T(8,128)(2,1)} %get-tuple-element.135), channel_id=1, source_target_pairs={{0,1},{1,2},{2,3},{3,4},{4,5},{5,6},{6,7},{7,0},{8,9},{9,10},{10,1... | collective-permute-start | bytes 6291464 | tf_op jit(solution)/shard_map/while/body/eval_jaxpr/ppermute | solution.py:40
  549.8 7.3 copy-start
  568.1 25.5 %collective-permute-start = (bf16[512,16,128]{2,0,1:T(8,128)(2,1)}, bf16[512,16,128]{2,0,1:T(8,128)(2,1)S(1)}, u32[]{:S(2)}, u32[]{:S(2)}) collective-permute-start(bf16[512,16,128]{2,0,1:T(8,128)(2,1)} %get-tuple-element.134), channel_id=1, source_target_pairs={{0,1},{1,2},{2,3},{3,4},{4,5},{5,6},{6,7},{7,0},{8,9},{9,10},{10,1... | collective-permute-start | bytes 6291464 | tf_op jit(solution)/shard_map/while/body/eval_jaxpr/ppermute | solution.py:39
  570.6 45.4 %collective-permute-start.1 = (bf16[512,16,128]{2,0,1:T(8,128)(2,1)}, bf16[512,16,128]{2,0,1:T(8,128)(2,1)}, u32[]{:S(2)}, u32[]{:S(2)}) collective-permute-start(bf16[512,16,128]{2,0,1:T(8,128)(2,1)} %get-tuple-element.135), channel_id=1, source_target_pairs={{0,1},{1,2},{2,3},{3,4},{4,5},{5,6},{6,7},{7,0},{8,9},{9,10},{10,1... | collective-permute-start | bytes 6291464 | tf_op jit(solution)/shard_map/while/body/eval_jaxpr/ppermute | solution.py:40
  611.9 7.3 copy-start
  (8 other events, 15.0 us)
Sparse Core Ops, SparseCore 0:
  8.9 84.4 all-gather.1
  655.6 152.8 reduce-scatter.1
where the time goes:
time: 820 us; the launch traced here: 819 us
  waiting for transfers between devices  420 us (51%)
  matrix products  243 us (30%)
  other arithmetic  72.6 us (9%)
  local copies, waits for them, and re-layouts  51.8 us (6%)
  starting transfers between devices  17.2 us (2%)
  between operations  13.6 us (2%)
    ppermute x7, waiting for transfers between devices, hop_step(): k_cur = lax.ppermute(k_cur, 'sp', hop_perm)  161 us
    reduce_scatter x1, waiting for transfers between devices, device_fn(): lax.psum_scatter(partial_sum, 'hp', scatter_dimension=0, tiled=True)  153 us
    all_gather x1, waiting for transfers between devices, device_fn(): x_full = lax.all_gather(x_loc, 'hp', axis=0, tiled=True)  86.1 us
    dot_general x8, matrix products, attend_block(): jnp.einsum('qhgd,khd->hgqk', q_heads, k_block, preferred_element_type=jnp...  75 us
    dot_general x8, matrix products, attend_block(): jnp.einsum('hgqk,khd->hgqd', prob_vals.astype(jnp.bfloat16), v_block, pre...  70.8 us
    reduce_sum x8, other arithmetic, attend_block(): new_sum = run_sum * correction + jnp.sum(prob_vals, axis=-1)  68.6 us
    while x49, local copies, waits for them, and re-layouts  44.8 us
    dot_general x1, matrix products, device_fn(): jnp.dot(x_full, w_q, preferred_element_type=jnp.float32)  25.8 us
  transfers between devices with their start and end apart: 16, of which 16 were waited for; matrix products, arithmetic and copies ran while one was open for 17% of the time, Pallas kernels for 0%

commit v1 on v0

v1 whole, which is shorter than its diff:
```python
import functools
import math

import jax
import jax.numpy as jnp
from jax import lax
from jax.experimental import pallas as pl
from jax.experimental.pallas import tpu as pltpu
from jax.sharding import PartitionSpec as P

HEAD_DIM = 128
CORES = 2
RING = 4
MESH_ID = pl.DeviceIdType.MESH
VMEM_BYTES = 64_000_000


def remote(src, dst, send_sem, recv_sem, sp, hp):
    return pltpu.make_async_remote_copy(
        src_ref=src, dst_ref=dst, send_sem=send_sem, recv_sem=recv_sem,
        device_id={'sp': sp, 'hp': hp}, device_id_type=MESH_ID)


def entry_barrier(peers):
    barrier = pltpu.get_barrier_semaphore()
    for sp, hp in peers:
        pl.semaphore_signal(barrier, inc=1, device_id={'sp': sp, 'hp': hp}, device_id_type=MESH_ID)
    pl.semaphore_wait(barrier, len(peers))


def qkv_kernel(x_ref, wq_ref, wk_ref, wv_ref, out_ref, xbuf, wbuf, obuf,
               own_send, relay_send, pair_send, load_sem, x_recv, w_sem, out_send, out_recv, out_local):
    sp, hp = lax.axis_index('sp'), lax.axis_index('hp')
    core, chip = lax.rem(sp, CORES), sp // CORES
    partner = sp + 1 - 2 * core
    up, down = lax.rem(hp + 1, RING), lax.rem(hp + RING - 1, RING)
    rows = x_ref.shape[0]
    half = rows // 2
    width = wbuf.shape[2] // 2
    mine, other = core * rows, (1 - core) * rows
    chips = [lax.rem(chip + d, RING) for d in range(RING)]
    ranks = [c * CORES + core for c in chips]

    def slot(p, base, side):
        return xbuf.at[p, pl.ds(pl.multiple_of(base + side * half, half), half)]

    def weight_copies(step, start):
        within = lax.rem(step, 6)
        buf = lax.rem(step, 3)
        for m, w_ref in enumerate((wq_ref, wk_ref, wv_ref)):
            for pair, dests in enumerate(((1, 3), (2, 0))):
                @pl.when(within == 2 * m + pair)
                def _():
                    for n, d in enumerate(dests):
                        cols = pl.ds(pl.multiple_of(ranks[d] * width, width), width)
                        copy = pltpu.make_async_copy(
                            w_ref.at[:, cols], wbuf.at[buf, :, pl.ds(n * width, width)], w_sem.at[buf, n])
                        copy.start() if start else copy.wait()

    weight_copies(0, True)
    weight_copies(1, True)
    own_load = pltpu.make_async_copy(x_ref, xbuf.at[0, pl.ds(pl.multiple_of(mine, rows), rows)], load_sem)
    own_load.start()

    entry_barrier([(partner, hp), (sp, up), (sp, down)] + [(ranks[d], hp) for d in (1, 2, 3)])

    first, second = x_ref.at[pl.ds(0, half)], x_ref.at[pl.ds(half, half)]
    own_copies = [
        remote(x_ref, xbuf.at[0, pl.ds(pl.multiple_of(mine, rows), rows)], own_send.at[0], x_recv.at[0, 1, 0], partner, hp),
        remote(first, slot(1, mine, 0), own_send.at[1], x_recv.at[1, 0, 0], sp, up),
        remote(second, slot(1, mine, 1), own_send.at[2], x_recv.at[1, 0, 1], sp, down),
        remote(second, slot(2, mine, 0), own_send.at[3], x_recv.at[2, 0, 0], sp, up),
        remote(first, slot(2, mine, 1), own_send.at[4], x_recv.at[2, 0, 1], sp, down),
    ]
    for copy in own_copies:
        copy.start()

    def from_side(p, side):
        return remote(slot(p, mine, side), slot(p, mine, side), own_send.at[0], x_recv.at[p, 0, side], sp, hp)

    def from_partner(p, side):
        return remote(slot(p, other, side), slot(p, other, side), own_send.at[0], x_recv.at[p, 1, side], sp, hp)

    def to_partner(p, side):
        return remote(slot(p, mine, side), slot(p, mine, side), pair_send.at[p - 1, side], x_recv.at[p, 1, side],
                      partner, hp)

    def relays():
        return [remote(slot(1, mine, 0), slot(3, mine, 0), relay_send.at[0], x_recv.at[3, 0, 0], sp, up),
                remote(slot(1, mine, 1), slot(3, mine, 1), relay_send.at[1], x_recv.at[3, 0, 1], sp, down)]

    def begin_pass(p):
        if p == 0:
            own_load.wait()
            whole = xbuf.at[0, pl.ds(pl.multiple_of(other, rows), rows)]
            remote(whole, whole, own_send.at[0], x_recv.at[0, 1, 0], sp, hp).wait_recv()
            return
        for side in (0, 1):
            from_side(p, side).wait_recv()
            if p == 1:
                relays()[side].start()
            to_partner(p, side).start()
        for side in (0, 1):
            from_partner(p, side).wait_recv()

    def send_out(step):
        p, within = step // 6, lax.rem(step, 6)
        for m in range(3):
            for pair, dests in enumerate(((1, 3), (2, 0))):
                @pl.when(within == 2 * m + pair)
                def _():
                    for n, d in enumerate(dests):
                        src, dst = obuf.at[step, n], out_ref.at[m, chip, p]
                        if d == 0:
                            pltpu.make_async_copy(src, dst, out_local).start()
                        else:
                            remote(src, dst, out_send, out_recv, ranks[d], hp).start()

    steps = 6 * RING

    def body(step, carry):
        for p in range(RING):
            @pl.when(step == 6 * p)
            def _():
                begin_pass(p)

        @pl.when(step + 2 < steps)
        def _():
            weight_copies(step + 2, True)

        weight_copies(step, False)
        buf = lax.rem(step, 3)
        prod = jnp.dot(xbuf[step // 6], wbuf[buf], preferred_element_type=jnp.float32).astype(jnp.bfloat16)
        obuf[step, 0] = prod[:, :width]
        obuf[step, 1] = prod[:, width:]

        @pl.when(step > 0)
        def _():
            send_out(step - 1)
        return carry

    lax.fori_loop(0, steps, body, 0)
    for copy in own_copies:
        copy.wait_send()
    for copy in relays():
        copy.wait_send()
    for p in (1, 2, 3):
        for side in (0, 1):
            to_partner(p, side).wait_send()
    send_out(jnp.int32(steps - 1))
    local_part, remote_part = obuf.at[pl.ds(0, 6)], obuf.at[pl.ds(0, 18)]
    pltpu.make_async_copy(local_part, local_part, out_local).wait()
    remote(remote_part, remote_part, out_send, out_recv, sp, hp).wait()


def attend_kernel(qkv_ref, o_ref, q_vm, k_vm, v_vm, vt_vm, s_even, s_odd, m_even, m_odd, o_vm,
                  load_sem, o_send, o_recv, o_local):
    sp, hp = lax.axis_index('sp'), lax.axis_index('hp')
    core, chip = lax.rem(sp, CORES), sp // CORES
    partner = sp + 1 - 2 * core
    blocks, block = q_vm.shape[0], q_vm.shape[1]
    rows, half = block // 2, block // 4
    scale = HEAD_DIM ** -0.5 * math.log2(math.e)
    strip = min(block, 32)

    loads = [pltpu.make_async_copy(qkv_ref.at[m], dst, load_sem.at[m]) for m, dst in enumerate((q_vm, k_vm, v_vm))]
    for copy in loads:
        copy.start()
    others = [(d, k) for d in range(RING) for k in range(CORES) if (d, k) != (0, 0)]
    rank_of = lambda d, k: lax.rem(chip + d, RING) * CORES + lax.rem(core + k, CORES)
    entry_barrier([(rank_of(d, k), hp) for d, k in others])
    for copy in loads:
        copy.wait()

    def turn(b, carry):
        vt_vm[b] = v_vm[b].astype(jnp.float32).T.astype(jnp.bfloat16)
        return carry

    lax.fori_loop(0, blocks, turn, 0)

    def which(i):
        return lax.rem(chip + 1 + lax.rem(i, RING), RING) * RING + lax.rem(i // RING + 1, RING)

    def lanes(head):
        return slice(head * HEAD_DIM, (head + 1) * HEAD_DIM)

    def scores(q_blk, head, chunk):
        return lax.dot_general(k_vm[chunk, :, lanes(head)], q_blk, (((1,), (1,)), ((), ())),
                               preferred_element_type=jnp.float32)

    def fold(x, op):
        parts = x.reshape(block // strip, strip, block)
        return op(parts, axis=0)

    def stage(q_next, next_head, s_next, m_next, s_now, m_now, head):
        shift = None if s_now is None else jnp.max(m_now[...], axis=0, keepdims=True) * scale
        peak = total = acc = None
        for chunk in range(blocks):
            s = scores(q_next, next_head, chunk)
            s_next[chunk] = s
            top = fold(s, jnp.max)
            peak = top if peak is None else jnp.maximum(peak, top)
            if s_now is not None:
                prob = jnp.exp2(s_now[chunk] * scale - shift)
                part = fold(prob, jnp.sum)
                total = part if total is None else total + part
                pv = jnp.dot(vt_vm[chunk, lanes(head), :], prob.astype(jnp.bfloat16), preferred_element_type=jnp.float32)
                acc = pv if acc is None else acc + pv
        m_next[...] = peak
        if s_now is None:
            return None
        return (acc / jnp.sum(total, axis=0, keepdims=True)).T.astype(jnp.bfloat16)

    stage(q_vm[which(0), :, lanes(0)], 0, s_even, m_even, None, None, 0)

    def send_home(i):
        d, p = lax.rem(i + 1, RING), lax.rem(i // RING + 1, RING)
        home = lax.rem(chip + d, RING) * CORES
        for pp in range(RING):
            @pl.when(p == pp)
            def _():
                for k in range(CORES):
                    kk = lax.rem(core + k, CORES)
                    for side in (0, 1):
                        target = (0, 1 + side, 1 + side, 3)[pp]
                        first = (1 - side if pp == 2 else side) * half
                        src = o_vm.at[i, pl.ds(pl.multiple_of(kk * rows + side * half, half), half)]
                        dst = o_ref.at[sp, target, pl.ds(first, half)]
                        if k:
                            remote(src, dst, o_send, o_recv, home + kk, hp).start()
                        else:
                            @pl.when(d == 0)
                            def _():
                                pltpu.make_async_copy(src, dst, o_local).start()

                            @pl.when(d != 0)
                            def _():
                                remote(src, dst, o_send, o_recv, home + kk, hp).start()

    def body(i, carry):
        now, later = which(i), which(lax.rem(i + 1, blocks))
        o_vm[i, :, lanes(0)] = stage(q_vm[now, :, lanes(1)], 1, s_odd, m_odd, s_even, m_even, 0)

        @pl.when(i > 0)
        def _():
            send_home(i - 1)
        o_vm[i, :, lanes(1)] = stage(q_vm[later, :, lanes(0)], 0, s_even, m_even, s_odd, m_odd, 1)
        return carry

    lax.fori_loop(0, blocks, body, 0)
    send_home(jnp.int32(blocks - 1))
    local_part = o_vm.at[pl.ds(0, 2)]
    pltpu.make_async_copy(local_part, local_part, o_local).wait()
    remote_part = o_vm.at[pl.ds(0, 14)]
    remote(remote_part, remote_part, o_send, o_recv, sp, hp).wait()


def project_kernel(o_ref, w_ref, y_ref, o_vm, wbuf, part, recv, load_sem, w_sem, send_sem, recv_sem):
    sp, hp = lax.axis_index('sp'), lax.axis_index('hp')
    ring = (lax.rem(hp + 1, RING), lax.rem(hp + RING - 1, RING))
    tiles, cols = part.shape[0], part.shape[3]
    ranks, _, rows, width = o_vm.shape

    def w_copy(tile):
        buf = lax.rem(tile, 3)
        return pltpu.make_async_copy(w_ref.at[:, pl.ds(pl.multiple_of(tile * cols, cols), cols)], wbuf.at[buf],
                                     w_sem.at[buf])

    load = pltpu.make_async_copy(o_ref, o_vm, load_sem)
    load.start()
    w_copy(0).start()
    w_copy(1).start()
    entry_barrier([(sp, ring[0]), (sp, ring[1])])
    load.wait()
    order = ((1, 3, 2), (2, 3, 1))

    def hop(tile, way, step):
        return remote(part.at[tile, order[way][step]], recv.at[tile, step], send_sem.at[tile, step],
                      recv_sem.at[tile, step], sp, ring[way])

    def compute(pair, carry):
        for way in (0, 1):
            tile = 2 * pair + way

            @pl.when(tile + 2 < tiles)
            def _():
                w_copy(tile + 2).start()
            w_copy(tile).wait()
            buf = lax.rem(tile, 3)
            acc = None
            for r in range(ranks):
                prod = jnp.dot(o_vm[r].reshape(RING * rows, width), wbuf[buf, pl.ds(r * width, width), :],
                               preferred_element_type=jnp.float32)
                acc = prod if acc is None else acc + prod
            part[tile] = acc.reshape(RING, rows, cols)

            @pl.when(tile > 0)
            def _():
                hop(tile - 1, 1 - way, 0).start()
        return carry

    lax.fori_loop(0, tiles // 2, compute, 0)
    hop(jnp.int32(tiles - 1), 1, 0).start()

    for step in (1, 2):
        def pass_on(pair, carry):
            for way in (0, 1):
                tile = 2 * pair + way
                hop(tile, way, step - 1).wait_recv()
                slot = order[way][step]
                part[tile, slot] = part[tile, slot] + recv[tile, step - 1]
            for way in (0, 1):
                hop(2 * pair + way, way, step).start()
            return carry

        lax.fori_loop(0, tiles // 2, pass_on, 0)

    def finish(pair, carry):
        for way in (0, 1):
            tile = 2 * pair + way
            hop(tile, way, 2).wait_recv()
            y_ref[:, pl.ds(pl.multiple_of(tile * cols, cols), cols)] = (part[tile, 0] + recv[tile, 2]).astype(y_ref.dtype)
        return carry

    lax.fori_loop(0, tiles // 2, finish, 0)

    def drain(pair, carry):
        for way in (0, 1):
            for step in range(3):
                hop(2 * pair + way, way, step).wait_send()
        return carry

    lax.fori_loop(0, tiles // 2, drain, 0)


def solution(mesh):
    assert mesh.shape['hp'] == RING and mesh.shape['sp'] == RING * CORES
    ranks = mesh.shape['sp']
    anywhere = pl.BlockSpec(memory_space=pl.ANY)
    dma = pltpu.SemaphoreType.DMA

    def params(ident):
        return pltpu.CompilerParams(collective_id=ident, has_side_effects=True, vmem_limit_bytes=VMEM_BYTES)

    def device_fn(x_loc, w_q, w_k, w_v, w_o):
        rows, depth = x_loc.shape
        width = w_q.shape[1] // ranks
        block = CORES * rows
        blocks = RING * RING
        bf16, f32 = jnp.bfloat16, jnp.float32
        tiles = 16
        cols = w_o.shape[1] // tiles

        qkv = pl.pallas_call(
            qkv_kernel,
            out_shape=jax.ShapeDtypeStruct((3, RING, RING, block, width), bf16),
            in_specs=[anywhere] * 4,
            out_specs=anywhere,
            scratch_shapes=[
                pltpu.VMEM((RING, block, depth), bf16),
                pltpu.VMEM((3, depth, 2 * width), bf16),
                pltpu.VMEM((6 * RING, 2, block, width), bf16),
                dma((5,)), dma((2,)), dma((3, 2)), dma, dma((RING, 2, 2)), dma((3, 2)), dma, dma, dma,
            ],
            compiler_params=params(0),
            name='gather_qkv',
        )(x_loc, w_q, w_k, w_v)

        heads_out = pl.pallas_call(
            attend_kernel,
            out_shape=jax.ShapeDtypeStruct((ranks, RING, rows, width), bf16),
            in_specs=[anywhere],
            out_specs=anywhere,
            scratch_shapes=[
                pltpu.VMEM((blocks, block, width), bf16),
                pltpu.VMEM((blocks, block, width), bf16),
                pltpu.VMEM((blocks, block, width), bf16),
                pltpu.VMEM((blocks, width, block), bf16),
                pltpu.VMEM((blocks, block, block), f32),
                pltpu.VMEM((blocks, block, block), f32),
                pltpu.VMEM((min(block, 32), block), f32),
                pltpu.VMEM((min(block, 32), block), f32),
                pltpu.VMEM((blocks, block, width), bf16),
                dma((3,)), dma, dma, dma,
            ],
            compiler_params=params(1),
            name='attend',
        )(qkv.reshape(3, blocks, block, width))

        return pl.pallas_call(
            project_kernel,
            out_shape=jax.ShapeDtypeStruct((rows, w_o.shape[1]), bf16),
            in_specs=[anywhere] * 2,
            out_specs=pl.BlockSpec(memory_space=pltpu.VMEM),
            scratch_shapes=[
                pltpu.VMEM((ranks, RING, rows, width), bf16),
                pltpu.VMEM((3, w_o.shape[0], cols), bf16),
                pltpu.VMEM((tiles, RING, rows, cols), f32),
                pltpu.VMEM((tiles, 3, rows, cols), f32),
                dma, dma((3,)), dma((tiles, 3)), dma((tiles, 3)),
            ],
            compiler_params=params(2),
            name='project',
        )(heads_out, w_o)

    seq_spec = P(('dp', 'sp', 'hp'), None)
    in_specs = (seq_spec, P(None, 'hp'), P(None, 'hp'), P(None, 'hp'), P('hp', None))
    return jax.shard_map(device_fn, mesh=mesh, in_specs=in_specs, out_specs=seq_spec, check_vma=False)
```

time: 820 us -> 303 us (0.37)
  waiting for transfers between devices: 420 us -> 0 us
  Pallas kernels: 0 us -> 299 us
  matrix products: 243 us -> 0 us
  other arithmetic: 72.6 us -> 0 us
  local copies, waits for them, and re-layouts: 51.8 us -> 3.1 us
  starting transfers between devices: 17.2 us -> 0 us
  between operations: 13.6 us -> 0.02 us
    pallas_call x0 -> x3, Pallas kernels: none -> 299 us  [the longest x1 145 us: device_fn(): pl.pallas_call(project_kernel, out_shape=jax.ShapeDtypeStruct((rows, w_o....]
    dot_general x20 -> x0, matrix products: 243 us -> none  [the longest x8 75 us: attend_block(): jnp.einsum('qhgd,khd->hgqk', q_heads, k_block, preferred_element_type=jnp...]
    ppermute x14 -> x0, waiting for transfers between devices: 181 us -> none  [the longest x7 161 us: hop_step(): k_cur = lax.ppermute(k_cur, 'sp', hop_perm)]
    reduce_scatter x1 -> x0, waiting for transfers between devices: 153 us -> none  [device_fn(): lax.psum_scatter(partial_sum, 'hp', scatter_dimension=0, tiled=True)]
    all_gather x1 -> x0, waiting for transfers between devices: 86.1 us -> none  [device_fn(): x_full = lax.all_gather(x_loc, 'hp', axis=0, tiled=True)]
    reduce_sum x8 -> x0, other arithmetic: 68.6 us -> none  [attend_block(): new_sum = run_sum * correction + jnp.sum(prob_vals, axis=-1)]
    while x51 -> x0, local copies, waits for them, and re-layouts: 49.9 us -> none
    ppermute x14 -> x0, starting transfers between devices: 17.2 us -> none  [the longest x7 17 us: hop_step(): k_cur = lax.ppermute(k_cur, 'sp', hop_perm)]
  transfers between devices with their start and end apart: 16 -> 0, of which waited for: 16 -> 0; matrix products, arithmetic and copies ran while one was open for 17% -> 0% of each run, Pallas kernels for 0% -> 0%
where the time goes in v1:
time: 303 us; the launch traced here: 302 us
  Pallas kernels  299 us (99%)
  local copies, waits for them, and re-layouts  3.1 us (1%)
    pallas_call x1, Pallas kernels, device_fn(): pl.pallas_call(project_kernel, out_shape=jax.ShapeDtypeStruct((rows, w_o....  145 us
    pallas_call x1, Pallas kernels, device_fn(): pl.pallas_call(qkv_kernel, out_shape=jax.ShapeDtypeStruct((3, RING, RING,...  105 us
    pallas_call x1, Pallas kernels, device_fn(): pl.pallas_call(attend_kernel, out_shape=jax.ShapeDtypeStruct((ranks, RING...  49.6 us

profile of v1, /device:TPU:97, one launch (start us, length us, event | category | flops | bytes accessed | tf_op | source)
XLA Modules:
  0.0 302.4 jit_solution(1835743558609718374)
XLA Ops:
  0.0 105.0 %gather_qkv.1 = bf16[3,4,4,256,256]{4,3,2,1,0:T(8,128)(2,1)} custom-call(bf16[128,8192]{1,0:T(8,128)(2,1)} %x_ref.1, bf16[8192,2048]{1,0:T(8,128)(2,1)} %wq_ref.1, bf16[8192,2048]{1,0:T(8,128)(2,1)} %wk_ref.1, bf16[8192,2048]{1,0:T(8,128)(2,1)} %wv_ref.1), custom_call_target="tpu_custom_call" | custom-call | tf_op jit(solution)/shard_map/gather_qkv/pallas_call | solution.py:354
  105.1 49.6 %attend.1.o_ref = bf16[8,4,128,256]{3,2,1,0:T(8,128)(2,1)} custom-call(bf16[3,16,256,256]{3,2,1,0:T(8,128)(2,1)} %bitcast.1), custom_call_target="tpu_custom_call" | custom-call | tf_op jit(solution)/shard_map/attend/pallas_call | solution.py:369
  154.7 144.6 %project.1 = bf16[128,8192]{1,0:T(8,128)(2,1)} custom-call(bf16[8,4,128,256]{3,2,1,0:T(8,128)(2,1)} %attend.1.o_ref, bf16[2048,8192]{1,0:T(8,128)(2,1)} %w_ref.1), custom_call_target="tpu_custom_call" | custom-call | tf_op jit(solution)/shard_map/project/pallas_call | solution.py:390
  299.3 3.1 %copy.7 = bf16[128,8192]{1,0:T(8,128)(2,1)} copy(bf16[128,8192]{1,0:T(8,128)(2,1)} %project.1) | data formatting | bytes 4194304

commit v2 on v1

v2 whole, which is shorter than its diff:
```python
import functools
import math

import jax
import jax.numpy as jnp
from jax import lax
from jax.experimental import pallas as pl
from jax.experimental.pallas import tpu as pltpu
from jax.sharding import PartitionSpec as P

HEAD_DIM = 128
CORES = 2
RING = 4
PAIRS = ((2, 0), (1, 3))
MESH_ID = pl.DeviceIdType.MESH
VMEM_BYTES = 66_000_000


def remote(src, dst, send_sem, recv_sem, sp, hp):
    return pltpu.make_async_remote_copy(
        src_ref=src, dst_ref=dst, send_sem=send_sem, recv_sem=recv_sem,
        device_id={'sp': sp, 'hp': hp}, device_id_type=MESH_ID)


def entry_barrier(peers):
    barrier = pltpu.get_barrier_semaphore()
    for sp, hp in peers:
        pl.semaphore_signal(barrier, inc=1, device_id={'sp': sp, 'hp': hp}, device_id_type=MESH_ID)
    pl.semaphore_wait(barrier, len(peers))


def qkv_kernel(x_ref, wq_ref, wk_ref, wv_ref, out_ref, xbuf, wbuf, obuf, via,
               own_send, relay_send, pair_send, load_sem, x_recv, w_sem, out_send, out_recv, out_local, via_recv, via_send):
    sp, hp = lax.axis_index('sp'), lax.axis_index('hp')
    core, chip = lax.rem(sp, CORES), sp // CORES
    partner = sp + 1 - 2 * core
    up, down = lax.rem(hp + 1, RING), lax.rem(hp + RING - 1, RING)
    rows = x_ref.shape[0]
    half = rows // 2
    width = wbuf.shape[2] // 2
    mine, other = core * rows, (1 - core) * rows
    chips = [lax.rem(chip + d, RING) for d in range(RING)]
    ranks = [c * CORES + core for c in chips]

    def slot(p, base, side):
        return xbuf.at[p, pl.ds(pl.multiple_of(base + side * half, half), half)]

    def weight_copies(step, start):
        within = lax.rem(step, 6)
        buf = lax.rem(step, 3)
        for m, w_ref in enumerate((wq_ref, wk_ref, wv_ref)):
            for pair, dests in enumerate(PAIRS):
                @pl.when(within == 3 * pair + m)
                def _():
                    for n, d in enumerate(dests):
                        cols = pl.ds(pl.multiple_of(ranks[d] * width, width), width)
                        copy = pltpu.make_async_copy(
                            w_ref.at[:, cols], wbuf.at[buf, :, pl.ds(n * width, width)], w_sem.at[buf, n])
                        copy.start() if start else copy.wait()

    weight_copies(0, True)
    weight_copies(1, True)
    own_load = pltpu.make_async_copy(x_ref, xbuf.at[0, pl.ds(pl.multiple_of(mine, rows), rows)], load_sem)
    own_load.start()

    entry_barrier([(partner, hp), (sp, up), (sp, down)] + [(ranks[d], hp) for d in (1, 2, 3)])

    first, second = x_ref.at[pl.ds(0, half)], x_ref.at[pl.ds(half, half)]
    own_copies = [
        remote(x_ref, xbuf.at[0, pl.ds(pl.multiple_of(mine, rows), rows)], own_send.at[0], x_recv.at[0, 1, 0], partner, hp),
        remote(first, slot(1, mine, 0), own_send.at[1], x_recv.at[1, 0, 0], sp, up),
        remote(second, slot(1, mine, 1), own_send.at[2], x_recv.at[1, 0, 1], sp, down),
        remote(second, slot(2, mine, 0), own_send.at[3], x_recv.at[2, 0, 0], sp, up),
        remote(first, slot(2, mine, 1), own_send.at[4], x_recv.at[2, 0, 1], sp, down),
    ]
    for copy in own_copies:
        copy.start()

    def from_side(p, side):
        return remote(slot(p, mine, side), slot(p, mine, side), own_send.at[0], x_recv.at[p, 0, side], sp, hp)

    def from_partner(p, side):
        return remote(slot(p, other, side), slot(p, other, side), own_send.at[0], x_recv.at[p, 1, side], sp, hp)

    def to_partner(p, side):
        return remote(slot(p, mine, side), slot(p, mine, side), pair_send.at[p - 1, side], x_recv.at[p, 1, side],
                      partner, hp)

    def relays():
        return [remote(slot(1, mine, 0), slot(3, mine, 0), relay_send.at[0], x_recv.at[3, 0, 0], sp, up),
                remote(slot(1, mine, 1), slot(3, mine, 1), relay_send.at[1], x_recv.at[3, 0, 1], sp, down)]

    def begin_pass(p):
        if p == 0:
            own_load.wait()
            whole = xbuf.at[0, pl.ds(pl.multiple_of(other, rows), rows)]
            remote(whole, whole, own_send.at[0], x_recv.at[0, 1, 0], sp, hp).wait_recv()
            return
        for side in (0, 1):
            from_side(p, side).wait_recv()
            if p == 1:
                relays()[side].start()
            to_partner(p, side).start()
        for side in (0, 1):
            from_partner(p, side).wait_recv()

    def send_out(step):
        p, within = step // 6, lax.rem(step, 6)
        for m in range(3):
            for pair, dests in enumerate(PAIRS):
                @pl.when(within == 3 * pair + m)
                def _():
                    for n, d in enumerate(dests):
                        src, dst = obuf.at[step, n], out_ref.at[m, chip, p]
                        if d == 0:
                            pltpu.make_async_copy(src, dst, out_local).start()
                        elif d == 2:
                            for way in (0, 1):
                                remote(src.at[pl.ds(way * rows, rows)], via.at[way, 3 * p + m], out_send,
                                       via_recv.at[way, 3 * p + m], ranks[1 + 2 * way], hp).start()
                        else:
                            remote(src, dst, out_send, out_recv, ranks[d], hp).start()

    def forward(p, m):
        for way in (0, 1):
            spot = via.at[way, 3 * p + m]
            remote(spot, spot, via_send, via_recv.at[way, 3 * p + m], sp, hp).wait_recv()
            remote(spot, out_ref.at[m, chips[3 - 2 * way], p, pl.ds(way * rows, rows)], via_send, out_recv,
                   ranks[1 + 2 * way], hp).start()

    steps = 6 * RING

    def body(step, carry):
        @pl.when(step + 2 < steps)
        def _():
            weight_copies(step + 2, True)

        for m in range(3):
            @pl.when((lax.rem(step + 2, 6) == m) & (step >= 4))
            def _():
                forward((step - 4) // 6, m)

        for p in range(RING):
            @pl.when(step == 6 * p)
            def _():
                begin_pass(p)

        weight_copies(step, False)
        buf = lax.rem(step, 3)
        prod = jnp.dot(xbuf[step // 6], wbuf[buf], preferred_element_type=jnp.float32).astype(jnp.bfloat16)
        obuf[step, 0] = prod[:, :width]
        obuf[step, 1] = prod[:, width:]

        @pl.when(step > 0)
        def _():
            send_out(step - 1)
        return carry

    lax.fori_loop(0, steps, body, 0)
    for copy in own_copies:
        copy.wait_send()
    for copy in relays():
        copy.wait_send()
    for p in (1, 2, 3):
        for side in (0, 1):
            to_partner(p, side).wait_send()
    send_out(jnp.int32(steps - 1))
    forward(RING - 1, 2)
    local_part, remote_part = obuf.at[pl.ds(0, 6)], obuf.at[pl.ds(0, 18)]
    pltpu.make_async_copy(local_part, local_part, out_local).wait()
    remote(remote_part, remote_part, out_send, out_recv, sp, hp).wait()
    remote(via, via, via_send, out_recv, sp, hp).wait_send()


def attend_project_kernel(qkv_ref, w_ref, y_ref, q_vm, k_vm, vt_vm, s_even, s_odd, m_even, m_odd, o_vm, o_rx, wbuf, part,
                          recv, load_sem, o_send, o_recv, w_sem, send_sem, recv_sem):
    sp, hp = lax.axis_index('sp'), lax.axis_index('hp')
    core, chip = lax.rem(sp, CORES), sp // CORES
    ring = (lax.rem(hp + 1, RING), lax.rem(hp + RING - 1, RING))
    blocks, block = q_vm.shape[0], q_vm.shape[1]
    rows, half = block // 2, block // 4
    ranks, width = o_rx.shape[1], o_rx.shape[3]
    tiles, cols = part.shape[0], part.shape[3]
    group = tiles // RING
    depth = wbuf.shape[0]
    scale = HEAD_DIM ** -0.5 * math.log2(math.e)
    strip = min(block, 32)

    loads = [pltpu.make_async_copy(qkv_ref.at[m], dst, load_sem.at[m]) for m, dst in enumerate((q_vm, k_vm, o_vm))]
    for copy in loads:
        copy.start()

    def w_copy(n):
        tile, buf = lax.rem(n, tiles), lax.rem(n, depth)
        return pltpu.make_async_copy(w_ref.at[:, pl.ds(pl.multiple_of(tile * cols, cols), cols)], wbuf.at[buf],
                                     w_sem.at[buf])

    for n in range(depth - 1):
        w_copy(jnp.int32(n)).start()
    others = [(d, k) for d in range(RING) for k in range(CORES) if (d, k) != (0, 0)]
    rank_of = lambda d, k: lax.rem(chip + d, RING) * CORES + lax.rem(core + k, CORES)
    entry_barrier([(rank_of(d, k), hp) for d, k in others] + [(sp, ring[0]), (sp, ring[1])])
    for copy in loads:
        copy.wait()

    def turn(b, carry):
        vt_vm[b] = o_vm[b].astype(jnp.float32).T.astype(jnp.bfloat16)
        return carry

    lax.fori_loop(0, blocks, turn, 0)

    def which(i):
        return lax.rem(chip + 1 + lax.rem(i, RING), RING) * RING + lax.rem(i // RING + 1, RING)

    def lanes(head):
        return slice(head * HEAD_DIM, (head + 1) * HEAD_DIM)

    def scores(q_blk, head, chunk):
        return lax.dot_general(k_vm[chunk, :, lanes(head)], q_blk, (((1,), (1,)), ((), ())),
                               preferred_element_type=jnp.float32)

    def fold(x, op):
        parts = x.reshape(block // strip, strip, block)
        return op(parts, axis=0)

    def stage(q_next, next_head, s_next, m_next, s_now, m_now, head):
        shift = None if s_now is None else jnp.max(m_now[...], axis=0, keepdims=True) * scale
        peak = total = acc = None
        for chunk in range(blocks):
            s = scores(q_next, next_head, chunk)
            s_next[chunk] = s
            top = fold(s, jnp.max)
            peak = top if peak is None else jnp.maximum(peak, top)
            if s_now is not None:
                prob = jnp.exp2(s_now[chunk] * scale - shift)
                add = fold(prob, jnp.sum)
                total = add if total is None else total + add
                pv = jnp.dot(vt_vm[chunk, lanes(head), :], prob.astype(jnp.bfloat16), preferred_element_type=jnp.float32)
                acc = pv if acc is None else acc + pv
        m_next[...] = peak
        if s_now is None:
            return None
        return (acc / jnp.sum(total, axis=0, keepdims=True)).T.astype(jnp.bfloat16)

    stage(q_vm[which(0), :, lanes(0)], 0, s_even, m_even, None, None, 0)

    def send_home(i):
        d, turn_no = lax.rem(i + 1, RING), i // RING
        home = lax.rem(chip + d, RING) * CORES
        for k in range(CORES):
            kk = lax.rem(core + k, CORES)
            piece = pl.ds(pl.multiple_of(kk * rows, rows), rows)

            def away():
                remote(o_vm.at[i, piece], o_rx.at[turn_no, sp], o_send, o_recv.at[turn_no], home + kk, hp).start()

            if k:
                away()
            else:
                pl.when(d != 0)(away)

                @pl.when(d == 0)
                def _():
                    o_rx[turn_no, sp] = o_vm[i, piece]

    order = ((1, 3, 2), (2, 3, 1))

    def hop(tile, way, step):
        return remote(part.at[tile, order[way][step]], recv.at[tile, step], send_sem.at[tile, step],
                      recv_sem.at[tile, step], sp, ring[way])

    def spot(turn_no, side):
        late, second = turn_no // 2, lax.rem(turn_no, 2)
        slot = (1 - late) * (1 + side) + late * (3 - 3 * second)
        first = (1 - late) * second * (1 - 2 * side) + side
        return slot, pl.ds(pl.multiple_of(first * half, half), half)

    def ship(n, way):
        turn_no, tile = n // tiles, lax.rem(n, tiles)

        @pl.when(turn_no < 2)
        def _():
            _, piece = spot(turn_no, way)
            remote(part.at[tile, order[way][0], piece], recv.at[tile, 0, piece], send_sem.at[tile, 0],
                   recv_sem.at[tile, 0], sp, ring[way]).start()

        @pl.when(turn_no == 2)
        def _():
            hop(tile, way, 1).start()

    def project(g):
        turn_no = g // RING

        @pl.when(lax.rem(g, RING) == 0)
        def _():
            seven = o_rx.at[turn_no, pl.ds(0, ranks - 1)]
            remote(seven, seven, o_send, o_recv.at[turn_no], sp, hp).wait_recv()

        for j in range(group):
            n, way = g * group + j, j % 2
            tile, buf = lax.rem(n, tiles), lax.rem(n, depth)

            @pl.when(n + depth - 1 < RING * tiles)
            def _():
                w_copy(n + depth - 1).start()
            w_copy(n).wait()
            acc = None
            for r in range(ranks):
                prod = jnp.dot(o_rx[turn_no, r], wbuf[buf, pl.ds(r * width, width), :],
                               preferred_element_type=jnp.float32)
                acc = prod if acc is None else acc + prod
            for side in (0, 1):
                slot, piece = spot(turn_no, side)
                part[tile, slot, piece] = acc[side * half:(side + 1) * half]

            @pl.when(turn_no == 2)
            def _():
                hop(tile, way, 0).wait_recv()
                part[tile, 3] = part[tile, 3] + recv[tile, 0]

            @pl.when(n > 0)
            def _():
                ship(n - 1, 1 - way)

    def body(i, carry):
        @pl.when(i > 0)
        def _():
            send_home(i - 1)
        now, later = which(i), which(lax.rem(i + 1, blocks))
        o_vm[i, :, lanes(0)] = stage(q_vm[now, :, lanes(1)], 1, s_odd, m_odd, s_even, m_even, 0)
        o_vm[i, :, lanes(1)] = stage(q_vm[later, :, lanes(0)], 0, s_even, m_even, s_odd, m_odd, 1)

        @pl.when(i >= RING)
        def _():
            project(i - RING)
        return carry

    lax.fori_loop(0, blocks, body, 0)
    send_home(jnp.int32(blocks - 1))

    def last_round(g, carry):
        project(g)
        return carry

    lax.fori_loop(blocks - RING, blocks, last_round, 0)

    def pass_on(pair, carry):
        for way in (0, 1):
            tile = 2 * pair + way
            hop(tile, way, 1).wait_recv()
            slot = order[way][2]
            part[tile, slot] = part[tile, slot] + recv[tile, 1]
        for way in (0, 1):
            hop(2 * pair + way, way, 2).start()
        return carry

    lax.fori_loop(0, tiles // 2, pass_on, 0)

    def finish(pair, carry):
        for way in (0, 1):
            tile = 2 * pair + way
            hop(tile, way, 2).wait_recv()
            y_ref[:, pl.ds(pl.multiple_of(tile * cols, cols), cols)] = (part[tile, 0] + recv[tile, 2]).astype(y_ref.dtype)
        return carry

    lax.fori_loop(0, tiles // 2, finish, 0)

    def drain(pair, carry):
        for way in (0, 1):
            for step in range(3):
                hop(2 * pair + way, way, step).wait_send()
        return carry

    lax.fori_loop(0, tiles // 2, drain, 0)
    away_part = o_vm.at[pl.ds(0, blocks - 2)]
    remote(away_part, away_part, o_send, o_recv.at[0], sp, hp).wait_send()


def solution(mesh):
    assert mesh.shape['hp'] == RING and mesh.shape['sp'] == RING * CORES
    ranks = mesh.shape['sp']
    anywhere = pl.BlockSpec(memory_space=pl.ANY)
    dma = pltpu.SemaphoreType.DMA

    def params(ident):
        return pltpu.CompilerParams(collective_id=ident, has_side_effects=True, vmem_limit_bytes=VMEM_BYTES)

    def device_fn(x_loc, w_q, w_k, w_v, w_o):
        rows, depth = x_loc.shape
        width = w_q.shape[1] // ranks
        block = CORES * rows
        blocks = RING * RING
        bf16, f32 = jnp.bfloat16, jnp.float32
        tiles = 16
        cols = w_o.shape[1] // tiles

        qkv = pl.pallas_call(
            qkv_kernel,
            out_shape=jax.ShapeDtypeStruct((3, RING, RING, block, width), bf16),
            in_specs=[anywhere] * 4,
            out_specs=anywhere,
            scratch_shapes=[
                pltpu.VMEM((RING, block, depth), bf16),
                pltpu.VMEM((3, depth, 2 * width), bf16),
                pltpu.VMEM((6 * RING, 2, block, width), bf16),
                pltpu.VMEM((2, 3 * RING, rows, width), bf16),
                dma((5,)), dma((2,)), dma((3, 2)), dma, dma((RING, 2, 2)), dma((3, 2)), dma, dma, dma,
                dma((2, 3 * RING)), dma,
            ],
            compiler_params=params(0),
            name='gather_qkv',
        )(x_loc, w_q, w_k, w_v)

        return pl.pallas_call(
            attend_project_kernel,
            out_shape=jax.ShapeDtypeStruct((rows, w_o.shape[1]), bf16),
            in_specs=[anywhere] * 2,
            out_specs=pl.BlockSpec(memory_space=pltpu.VMEM),
            scratch_shapes=[
                pltpu.VMEM((blocks, block, width), bf16),
                pltpu.VMEM((blocks, block, width), bf16),
                pltpu.VMEM((blocks, width, block), bf16),
                pltpu.VMEM((blocks, block, block), f32),
                pltpu.VMEM((blocks, block, block), f32),
                pltpu.VMEM((min(block, 32), block), f32),
                pltpu.VMEM((min(block, 32), block), f32),
                pltpu.VMEM((blocks, block, width), bf16),
                pltpu.VMEM((RING, ranks, rows, width), bf16),
                pltpu.VMEM((4, w_o.shape[0], cols), bf16),
                pltpu.VMEM((tiles, RING, rows, cols), f32),
                pltpu.VMEM((tiles, 3, rows, cols), f32),
                dma((3,)), dma, dma((RING,)), dma((4,)), dma((tiles, 3)), dma((tiles, 3)),
            ],
            compiler_params=params(1),
            name='attend_project',
        )(qkv.reshape(3, blocks, block, width), w_o)

    seq_spec = P(('dp', 'sp', 'hp'), None)
    in_specs = (seq_spec, P(None, 'hp'), P(None, 'hp'), P(None, 'hp'), P('hp', None))
    return jax.shard_map(device_fn, mesh=mesh, in_specs=in_specs, out_specs=seq_spec, check_vma=False)
```

time: 303 us -> 273 us (0.901)
  Pallas kernels: 299 us -> 269 us
    pallas_call x2 -> x1, Pallas kernels: 194 us -> 163 us  [device_fn(): pl.pallas_call(attend_project_kernel, out_shape=jax.ShapeDtypeStruct((row...]
where the time goes in v2:
time: 273 us
  Pallas kernels  269 us (99%)
  local copies, waits for them, and re-layouts  3.1 us (1%)
    pallas_call x1, Pallas kernels, device_fn(): pl.pallas_call(attend_project_kernel, out_shape=jax.ShapeDtypeStruct((row...  163 us
    pallas_call x1, Pallas kernels, device_fn(): pl.pallas_call(qkv_kernel, out_shape=jax.ShapeDtypeStruct((3, RING, RING,...  106 us

profile of v2, /device:TPU:97, one launch (start us, length us, event | category | flops | bytes accessed | tf_op | source)
XLA Modules:
  0.0 272.6 jit_solution(8464898553477534750)
XLA Ops:
  0.0 106.4 %gather_qkv.1 = bf16[3,4,4,256,256]{4,3,2,1,0:T(8,128)(2,1)} custom-call(bf16[128,8192]{1,0:T(8,128)(2,1)} %x_ref.1, bf16[8192,2048]{1,0:T(8,128)(2,1)} %wq_ref.1, bf16[8192,2048]{1,0:T(8,128)(2,1)} %wk_ref.1, bf16[8192,2048]{1,0:T(8,128)(2,1)} %wv_ref.1), custom_call_target="tpu_custom_call" | custom-call | tf_op jit(solution)/shard_map/gather_qkv/pallas_call | solution.py:397
  106.4 163.0 %attend_project.1 = bf16[128,8192]{1,0:T(8,128)(2,1)} custom-call(bf16[3,16,256,256]{3,2,1,0:T(8,128)(2,1)} %bitcast.1, bf16[2048,8192]{1,0:T(8,128)(2,1)} %w_ref.1), custom_call_target="tpu_custom_call" | custom-call | tf_op jit(solution)/shard_map/attend_project/pallas_call | solution.py:414
  269.5 3.1 %copy.7 = bf16[128,8192]{1,0:T(8,128)(2,1)} copy(bf16[128,8192]{1,0:T(8,128)(2,1)} %attend_project.1) | data formatting | bytes 4194304

commit v3 on v2

--- a/solution.py
+++ b/solution.py
@@ -11,7 +11,6 @@
 HEAD_DIM = 128
 CORES = 2
 RING = 4
-PAIRS = ((2, 0), (1, 3))
 MESH_ID = pl.DeviceIdType.MESH
 VMEM_BYTES = 66_000_000
 
@@ -29,37 +28,50 @@
     pl.semaphore_wait(barrier, len(peers))
 
 
-def qkv_kernel(x_ref, wq_ref, wk_ref, wv_ref, out_ref, xbuf, wbuf, obuf, via,
+def qkv_kernel(x_ref, wq_ref, wk_ref, wv_ref, out_ref, xbuf, wbuf, acc_vm, obuf, via,
                own_send, relay_send, pair_send, load_sem, x_recv, w_sem, out_send, out_recv, out_local, via_recv, via_send):
     sp, hp = lax.axis_index('sp'), lax.axis_index('hp')
     core, chip = lax.rem(sp, CORES), sp // CORES
     partner = sp + 1 - 2 * core
     up, down = lax.rem(hp + 1, RING), lax.rem(hp + RING - 1, RING)
-    rows = x_ref.shape[0]
-    half = rows // 2
-    width = wbuf.shape[2] // 2
+    rows, depth = x_ref.shape
+    half, deep = rows // 2, depth // 2
+    units, width = wbuf.shape[0], wbuf.shape[2] // 2
     mine, other = core * rows, (1 - core) * rows
     chips = [lax.rem(chip + d, RING) for d in range(RING)]
     ranks = [c * CORES + core for c in chips]
+    weights = (wv_ref, wk_ref, wq_ref)
+    last = 2 * (RING - 1) * 3
 
     def slot(p, base, side):
-        return xbuf.at[p, pl.ds(pl.multiple_of(base + side * half, half), half)]
-
-    def weight_copies(step, start):
-        within = lax.rem(step, 6)
-        buf = lax.rem(step, 3)
-        for m, w_ref in enumerate((wq_ref, wk_ref, wv_ref)):
-            for pair, dests in enumerate(PAIRS):
-                @pl.when(within == 3 * pair + m)
-                def _():
-                    for n, d in enumerate(dests):
-                        cols = pl.ds(pl.multiple_of(ranks[d] * width, width), width)
-                        copy = pltpu.make_async_copy(
-                            w_ref.at[:, cols], wbuf.at[buf, :, pl.ds(n * width, width)], w_sem.at[buf, n])
-                        copy.start() if start else copy.wait()
-
-    weight_copies(0, True)
-    weight_copies(1, True)
+        at = pl.ds(pl.multiple_of(base + side * half, half), half)
+        if p < 3:
+            return xbuf.at[p, at]
+        return xbuf.at[3, at, pl.ds((p - 3) * deep, deep)]
+
+    def unit_copies(u, m, pair, part):
+        buf = lax.rem(u, units)
+        for n in range(2):
+            rank = lax.rem(chip + (2 - pair if n == 0 else 3 * pair), RING) * CORES + core
+            yield pltpu.make_async_copy(
+                weights[m].at[pl.ds(part * deep, deep), pl.ds(pl.multiple_of(rank * width, width), width)],
+                wbuf.at[buf, :, pl.ds(n * width, width)], w_sem.at[buf, n])
+
+    def start_units(step, m, pair):
+        for part in range(2):
+            for copy in unit_copies(2 * step + part, m, pair, part):
+                copy.start()
+
+    def start_far_unit(u, m, pair, part):
+        for copy in unit_copies(u, m, pair, part):
+            copy.start()
+
+    def wait_unit(u):
+        for copy in unit_copies(u, 0, 0, 0):
+            copy.wait()
+
+    start_units(jnp.int32(0), 0, 0)
+    start_units(jnp.int32(1), 1, 0)
     own_load = pltpu.make_async_copy(x_ref, xbuf.at[0, pl.ds(pl.multiple_of(mine, rows), rows)], load_sem)
     own_load.start()
 
@@ -67,28 +79,27 @@
 
     first, second = x_ref.at[pl.ds(0, half)], x_ref.at[pl.ds(half, half)]
     own_copies = [
-        remote(x_ref, xbuf.at[0, pl.ds(pl.multiple_of(mine, rows), rows)], own_send.at[0], x_recv.at[0, 1, 0], partner, hp),
         remote(first, slot(1, mine, 0), own_send.at[1], x_recv.at[1, 0, 0], sp, up),
         remote(second, slot(1, mine, 1), own_send.at[2], x_recv.at[1, 0, 1], sp, down),
+        remote(x_ref, xbuf.at[0, pl.ds(pl.multiple_of(mine, rows), rows)], own_send.at[0], x_recv.at[0, 1, 0], partner, hp),
         remote(second, slot(2, mine, 0), own_send.at[3], x_recv.at[2, 0, 0], sp, up),
         remote(first, slot(2, mine, 1), own_send.at[4], x_recv.at[2, 0, 1], sp, down),
     ]
     for copy in own_copies:
         copy.start()
 
-    def from_side(p, side):
-        return remote(slot(p, mine, side), slot(p, mine, side), own_send.at[0], x_recv.at[p, 0, side], sp, hp)
-
-    def from_partner(p, side):
-        return remote(slot(p, other, side), slot(p, other, side), own_send.at[0], x_recv.at[p, 1, side], sp, hp)
+    def arrived(p, k, side):
+        place = slot(p, mine if k == 0 else other, side)
+        return remote(place, place, own_send.at[0], x_recv.at[p, k, side], sp, hp)
 
     def to_partner(p, side):
         return remote(slot(p, mine, side), slot(p, mine, side), pair_send.at[p - 1, side], x_recv.at[p, 1, side],
                       partner, hp)
 
-    def relays():
-        return [remote(slot(1, mine, 0), slot(3, mine, 0), relay_send.at[0], x_recv.at[3, 0, 0], sp, up),
-                remote(slot(1, mine, 1), slot(3, mine, 1), relay_send.at[1], x_recv.at[3, 0, 1], sp, down)]
+    def relay(part, side):
+        at = pl.ds(pl.multiple_of(mine + side * half, half), half)
+        return remote(xbuf.at[1, at, pl.ds(part * deep, deep)], slot(3 + part, mine, side), relay_send.at[part, side],
+                      x_recv.at[3 + part, 0, side], sp, (up, down)[side])
 
     def begin_pass(p):
         if p == 0:
@@ -97,77 +108,148 @@
             remote(whole, whole, own_send.at[0], x_recv.at[0, 1, 0], sp, hp).wait_recv()
             return
         for side in (0, 1):
-            from_side(p, side).wait_recv()
+            arrived(p, 0, side).wait_recv()
             if p == 1:
-                relays()[side].start()
+                for part in range(2):
+                    relay(part, side).start()
             to_partner(p, side).start()
         for side in (0, 1):
-            from_partner(p, side).wait_recv()
-
-    def send_out(step):
-        p, within = step // 6, lax.rem(step, 6)
-        for m in range(3):
-            for pair, dests in enumerate(PAIRS):
-                @pl.when(within == 3 * pair + m)
-                def _():
-                    for n, d in enumerate(dests):
-                        src, dst = obuf.at[step, n], out_ref.at[m, chip, p]
-                        if d == 0:
-                            pltpu.make_async_copy(src, dst, out_local).start()
-                        elif d == 2:
-                            for way in (0, 1):
-                                remote(src.at[pl.ds(way * rows, rows)], via.at[way, 3 * p + m], out_send,
-                                       via_recv.at[way, 3 * p + m], ranks[1 + 2 * way], hp).start()
-                        else:
-                            remote(src, dst, out_send, out_recv, ranks[d], hp).start()
+            arrived(p, 1, side).wait_recv()
+
+    def send_out(g, m):
+        p, matrix = g // 2, 2 - m
+
+        @pl.when(lax.rem(g, 2) == 0)
+        def _():
+            for way in (0, 1):
+                remote(obuf.at[g, m, 0, pl.ds(way * rows, rows)], via.at[way, 3 * p + m], out_send,
+                       via_recv.at[way, 3 * p + m], ranks[1 + 2 * way], hp).start()
+            pltpu.make_async_copy(obuf.at[g, m, 1], out_ref.at[matrix, chip, p], out_local).start()
+
+        @pl.when(lax.rem(g, 2) == 1)
+        def _():
+            for n, d in enumerate((1, 3)):
+                remote(obuf.at[g, m, n], out_ref.at[matrix, chip, p], out_send, out_recv, ranks[d], hp).start()
 
     def forward(p, m):
         for way in (0, 1):
             spot = via.at[way, 3 * p + m]
             remote(spot, spot, via_send, via_recv.at[way, 3 * p + m], sp, hp).wait_recv()
-            remote(spot, out_ref.at[m, chips[3 - 2 * way], p, pl.ds(way * rows, rows)], via_send, out_recv,
+            remote(spot, out_ref.at[2 - m, chips[3 - 2 * way], p, pl.ds(way * rows, rows)], via_send, out_recv,
                    ranks[1 + 2 * way], hp).start()
 
-    steps = 6 * RING
-
-    def body(step, carry):
-        @pl.when(step + 2 < steps)
-        def _():
-            weight_copies(step + 2, True)
-
+    def keep(g, m, prod):
+        for n in range(2):
+            blk = prod[:, n * width:(n + 1) * width]
+            if m == 0:
+                blk = blk.T
+            obuf[g, m, n] = blk.astype(jnp.bfloat16)
+
+    def settle(g, m):
+        if m:
+            send_out(g, m - 1)
+
+            @pl.when(lax.rem(g, 2) == 1)
+            def _():
+                forward(g // 2, m - 1)
+        else:
+            @pl.when(g > 0)
+            def _():
+                send_out(g - 1, 2)
+
+            @pl.when((g > 0) & (lax.rem(g, 2) == 0))
+            def _():
+                forward(g // 2 - 1, 2)
+
+    def full_steps(g, carry):
+        p, pair = g // 2, lax.rem(g, 2)
         for m in range(3):
-            @pl.when((lax.rem(step + 2, 6) == m) & (step >= 4))
-            def _():
-                forward((step - 4) // 6, m)
-
-        for p in range(RING):
-            @pl.when(step == 6 * p)
-            def _():
-                begin_pass(p)
-
-        weight_copies(step, False)
-        buf = lax.rem(step, 3)
-        prod = jnp.dot(xbuf[step // 6], wbuf[buf], preferred_element_type=jnp.float32).astype(jnp.bfloat16)
-        obuf[step, 0] = prod[:, :width]
-        obuf[step, 1] = prod[:, width:]
-
-        @pl.when(step > 0)
-        def _():
-            send_out(step - 1)
+            step = 3 * g + m
+            far = step + 2 - last
+            ahead, ahead_m = (step + 2) // 3, (m + 2) % 3
+
+            @pl.when(far < 0)
+            def _():
+                start_units(step + 2, ahead_m, lax.rem(ahead, 2))
+            if m:
+                @pl.when(far >= 0)
+                def _():
+                    for n in range(2):
+                        start_far_unit(2 * last + 2 * (m - 1) + n, (2 * (m - 1) + n) % 3, (2 * (m - 1) + n) // 3, 0)
+            if m == 0:
+                for q in range(3):
+                    @pl.when(g == 2 * q)
+                    def _():
+                        begin_pass(q)
+            wait_unit(2 * step)
+            wait_unit(2 * step + 1)
+            buf = lax.rem(2 * step, units)
+            prod = (jnp.dot(xbuf[p, :, :deep], wbuf[buf], preferred_element_type=jnp.float32)
+                    + jnp.dot(xbuf[p, :, deep:], wbuf[buf + 1], preferred_element_type=jnp.float32))
+            keep(g, m, prod)
+            settle(g, m)
         return carry
 
-    lax.fori_loop(0, steps, body, 0)
+    lax.fori_loop(0, 2 * (RING - 1), full_steps, 0)
+
+    for part in range(2):
+        def far_steps(pair, carry):
+            g = 2 * (RING - 1) + pair
+            for m in range(3):
+                t = 6 * part + 3 * pair + m
+                nxt = t + 4
+                nxt_m = (m + 1) % 3
+
+                @pl.when(nxt < 12)
+                def _():
+                    if part == 0:
+                        within = lax.rem(nxt, 6)
+                        for h in range(2):
+                            @pl.when(nxt // 6 == h)
+                            def _():
+                                start_far_unit(2 * last + nxt, nxt_m, within // 3, h)
+                    else:
+                        start_far_unit(2 * last + nxt, nxt_m, lax.rem(nxt, 6) // 3, 1)
+                if m == 0:
+                    @pl.when(pair == 0)
+                    def _():
+                        begin_pass(3 + part)
+                u = 2 * last + t
+                wait_unit(u)
+                prod = jnp.dot(xbuf[3, :, part * deep:(part + 1) * deep], wbuf[lax.rem(u, units)],
+                               preferred_element_type=jnp.float32)
+                if part == 0:
+                    acc_vm[pair, m] = prod
+                    if m == 0:
+                        @pl.when(pair == 0)
+                        def _():
+                            send_out(2 * (RING - 1) - 1, 2)
+                            forward(RING - 2, 2)
+                else:
+                    keep(g, m, acc_vm[pair, m] + prod)
+                    if m:
+                        settle(g, m)
+                    else:
+                        @pl.when(pair == 1)
+                        def _():
+                            send_out(g - 1, 2)
+            return carry
+
+        lax.fori_loop(0, 2, far_steps, 0)
+
     for copy in own_copies:
         copy.wait_send()
-    for copy in relays():
-        copy.wait_send()
-    for p in (1, 2, 3):
+    send_out(jnp.int32(2 * RING - 1), 2)
+    forward(RING - 1, 2)
+    for part in range(2):
+        for side in (0, 1):
+            relay(part, side).wait_send()
+    for p in (1, 2, 3, 4):
         for side in (0, 1):
             to_partner(p, side).wait_send()
-    send_out(jnp.int32(steps - 1))
-    forward(RING - 1, 2)
-    local_part, remote_part = obuf.at[pl.ds(0, 6)], obuf.at[pl.ds(0, 18)]
+    local_part = obuf.at[pl.ds(0, RING // 2), :, :]
     pltpu.make_async_copy(local_part, local_part, out_local).wait()
+    remote_part = obuf.at[pl.ds(0, 3 * RING // 2), :, :]
     remote(remote_part, remote_part, out_send, out_recv, sp, hp).wait()
     remote(via, via, via_send, out_recv, sp, hp).wait_send()
 
@@ -181,12 +263,13 @@
     rows, half = block // 2, block // 4
     ranks, width = o_rx.shape[1], o_rx.shape[3]
     tiles, cols = part.shape[0], part.shape[3]
-    group = tiles // RING
+    lag = blocks // RING
+    per_block = tiles // (2 * lag)
     depth = wbuf.shape[0]
     scale = HEAD_DIM ** -0.5 * math.log2(math.e)
     strip = min(block, 32)
 
-    loads = [pltpu.make_async_copy(qkv_ref.at[m], dst, load_sem.at[m]) for m, dst in enumerate((q_vm, k_vm, o_vm))]
+    loads = [pltpu.make_async_copy(qkv_ref.at[m], dst, load_sem.at[m]) for m, dst in enumerate((q_vm, k_vm, vt_vm))]
     for copy in loads:
         copy.start()
 
@@ -202,12 +285,6 @@
     entry_barrier([(rank_of(d, k), hp) for d, k in others] + [(sp, ring[0]), (sp, ring[1])])
     for copy in loads:
         copy.wait()
-
-    def turn(b, carry):
-        vt_vm[b] = o_vm[b].astype(jnp.float32).T.astype(jnp.bfloat16)
-        return carry
-
-    lax.fori_loop(0, blocks, turn, 0)
 
     def which(i):
         return lax.rem(chip + 1 + lax.rem(i, RING), RING) * RING + lax.rem(i // RING + 1, RING)
@@ -288,16 +365,16 @@
         def _():
             hop(tile, way, 1).start()
 
-    def project(g):
-        turn_no = g // RING
-
-        @pl.when(lax.rem(g, RING) == 0)
+    def project(pair):
+        turn_no = pair // (tiles // 2)
+
+        @pl.when(lax.rem(pair, tiles // 2) == 0)
         def _():
             seven = o_rx.at[turn_no, pl.ds(0, ranks - 1)]
             remote(seven, seven, o_send, o_recv.at[turn_no], sp, hp).wait_recv()
 
-        for j in range(group):
-            n, way = g * group + j, j % 2
+        for way in (0, 1):
+            n = 2 * pair + way
             tile, buf = lax.rem(n, tiles), lax.rem(n, depth)
 
             @pl.when(n + depth - 1 < RING * tiles)
@@ -328,21 +405,25 @@
             send_home(i - 1)
         now, later = which(i), which(lax.rem(i + 1, blocks))
         o_vm[i, :, lanes(0)] = stage(q_vm[now, :, lanes(1)], 1, s_odd, m_odd, s_even, m_even, 0)
+
+        @pl.when(i >= lag)
+        def _():
+            project(per_block * (i - lag))
         o_vm[i, :, lanes(1)] = stage(q_vm[later, :, lanes(0)], 0, s_even, m_even, s_odd, m_odd, 1)
 
-        @pl.when(i >= RING)
-        def _():
-            project(i - RING)
+        @pl.when(i >= lag)
+        def _():
+            project(per_block * (i - lag) + 1)
         return carry
 
     lax.fori_loop(0, blocks, body, 0)
     send_home(jnp.int32(blocks - 1))
 
-    def last_round(g, carry):
-        project(g)
+    def last_round(pair, carry):
+        project(pair)
         return carry
 
-    lax.fori_loop(blocks - RING, blocks, last_round, 0)
+    lax.fori_loop(per_block * (blocks - lag), per_block * blocks, last_round, 0)
 
     def pass_on(pair, carry):
         for way in (0, 1):
@@ -389,6 +470,7 @@
         rows, depth = x_loc.shape
         width = w_q.shape[1] // ranks
         block = CORES * rows
+        assert block == width
         blocks = RING * RING
         bf16, f32 = jnp.bfloat16, jnp.float32
         tiles = 16
@@ -401,10 +483,11 @@
             out_specs=anywhere,
             scratch_shapes=[
                 pltpu.VMEM((RING, block, depth), bf16),
-                pltpu.VMEM((3, depth, 2 * width), bf16),
-                pltpu.VMEM((6 * RING, 2, block, width), bf16),
+                pltpu.VMEM((6, depth // 2, 2 * width), bf16),
+                pltpu.VMEM((2, 3, block, 2 * width), f32),
+                pltpu.VMEM((2 * RING, 3, 2, block, width), bf16),
                 pltpu.VMEM((2, 3 * RING, rows, width), bf16),
-                dma((5,)), dma((2,)), dma((3, 2)), dma, dma((RING, 2, 2)), dma((3, 2)), dma, dma, dma,
+                dma((5,)), dma((2, 2)), dma((4, 2)), dma, dma((RING + 1, 2, 2)), dma((6, 2)), dma, dma, dma,
                 dma((2, 3 * RING)), dma,
             ],
             compiler_params=params(0),

time: 273 us -> 269 us (0.985)
  Pallas kernels: 269 us -> 265 us
    pallas_call x1, Pallas kernels: 163 us -> 158 us  [device_fn(): pl.pallas_call(attend_project_kernel, out_shape=jax.ShapeDtypeStruct((row...]
where the time goes in v3:
time: 269 us
  Pallas kernels  265 us (99%)
  local copies, waits for them, and re-layouts  3.1 us (1%)
    pallas_call x1, Pallas kernels, device_fn(): pl.pallas_call(attend_project_kernel, out_shape=jax.ShapeDtypeStruct((row...  158 us
    pallas_call x1, Pallas kernels, device_fn(): pl.pallas_call(qkv_kernel, out_shape=jax.ShapeDtypeStruct((3, RING, RING,...  108 us

profile of v3, /device:TPU:97, one launch (start us, length us, event | category | flops | bytes accessed | tf_op | source)
XLA Modules:
  0.0 268.6 jit_solution(14185586317658211339)
XLA Ops:
  0.0 107.8 %gather_qkv.1 = bf16[3,4,4,256,256]{4,3,2,1,0:T(8,128)(2,1)} custom-call(bf16[128,8192]{1,0:T(8,128)(2,1)} %x_ref.1, bf16[8192,2048]{1,0:T(8,128)(2,1)} %wq_ref.1, bf16[8192,2048]{1,0:T(8,128)(2,1)} %wk_ref.1, bf16[8192,2048]{1,0:T(8,128)(2,1)} %wv_ref.1), custom_call_target="tpu_custom_call" | custom-call | tf_op jit(solution)/shard_map/gather_qkv/pallas_call | solution.py:479
  107.8 157.6 %attend_project.1 = bf16[128,8192]{1,0:T(8,128)(2,1)} custom-call(bf16[3,16,256,256]{3,2,1,0:T(8,128)(2,1)} %bitcast.1, bf16[2048,8192]{1,0:T(8,128)(2,1)} %w_ref.1), custom_call_target="tpu_custom_call" | custom-call | tf_op jit(solution)/shard_map/attend_project/pallas_call | solution.py:497
  265.5 3.1 %copy.7 = bf16[128,8192]{1,0:T(8,128)(2,1)} copy(bf16[128,8192]{1,0:T(8,128)(2,1)} %attend_project.1) | data formatting | bytes 4194304

commit v4 on v3

--- a/solution.py
+++ b/solution.py
@@ -283,7 +283,7 @@
     others = [(d, k) for d in range(RING) for k in range(CORES) if (d, k) != (0, 0)]
     rank_of = lambda d, k: lax.rem(chip + d, RING) * CORES + lax.rem(core + k, CORES)
     entry_barrier([(rank_of(d, k), hp) for d, k in others] + [(sp, ring[0]), (sp, ring[1])])
-    for copy in loads:
+    for copy in loads[:2]:
         copy.wait()
 
     def which(i):
@@ -320,6 +320,7 @@
         return (acc / jnp.sum(total, axis=0, keepdims=True)).T.astype(jnp.bfloat16)
 
     stage(q_vm[which(0), :, lanes(0)], 0, s_even, m_even, None, None, 0)
+    loads[2].wait()
 
     def send_home(i):
         d, turn_no = lax.rem(i + 1, RING), i // RING
@@ -394,10 +395,8 @@
             def _():
                 hop(tile, way, 0).wait_recv()
                 part[tile, 3] = part[tile, 3] + recv[tile, 0]
-
-            @pl.when(n > 0)
-            def _():
-                ship(n - 1, 1 - way)
+        for way in (0, 1):
+            ship(2 * pair + way, way)
 
     def body(i, carry):
         @pl.when(i > 0)

time: 269 us -> 266 us (0.989)
  no operation moved by 1% of the time
where the time goes in v4:
time: 266 us
  Pallas kernels  263 us (99%)
  local copies, waits for them, and re-layouts  3.1 us (1%)
    pallas_call x1, Pallas kernels, device_fn(): pl.pallas_call(attend_project_kernel, out_shape=jax.ShapeDtypeStruct((row...  155 us
    pallas_call x1, Pallas kernels, device_fn(): pl.pallas_call(qkv_kernel, out_shape=jax.ShapeDtypeStruct((3, RING, RING,...  108 us

profile of v4, /device:TPU:97, one launch (start us, length us, event | category | flops | bytes accessed | tf_op | source)
XLA Modules:
  0.0 266.2 jit_solution(8880846661701765484)
XLA Ops:
  0.0 107.8 %gather_qkv.1 = bf16[3,4,4,256,256]{4,3,2,1,0:T(8,128)(2,1)} custom-call(bf16[128,8192]{1,0:T(8,128)(2,1)} %x_ref.1, bf16[8192,2048]{1,0:T(8,128)(2,1)} %wq_ref.1, bf16[8192,2048]{1,0:T(8,128)(2,1)} %wk_ref.1, bf16[8192,2048]{1,0:T(8,128)(2,1)} %wv_ref.1), custom_call_target="tpu_custom_call" | custom-call | tf_op jit(solution)/shard_map/gather_qkv/pallas_call | solution.py:478
  107.8 155.3 %attend_project.1 = bf16[128,8192]{1,0:T(8,128)(2,1)} custom-call(bf16[3,16,256,256]{3,2,1,0:T(8,128)(2,1)} %bitcast.1, bf16[2048,8192]{1,0:T(8,128)(2,1)} %w_ref.1), custom_call_target="tpu_custom_call" | custom-call | tf_op jit(solution)/shard_map/attend_project/pallas_call | solution.py:496
  263.1 3.1 %copy.7 = bf16[128,8192]{1,0:T(8,128)(2,1)} copy(bf16[128,8192]{1,0:T(8,128)(2,1)} %attend_project.1) | data formatting | bytes 4194304
